TPU v7x, 32 devices: a whole 2x2x4 slice. The times are simulated.
32 devices in a mesh: sec: 8 (over y, x, core), pan: 4 (over z).
Axes of the slice: x: 2, y: 2, z: 4, core: 2. Of those that a mesh axis runs over, the one named last changes fastest.
Arguments:
- wave_state: bfloat16 [8, 512, 512], P('sec', 'pan'), may hold values from -6 to 6
- right_blocks: bfloat16 [8, 16, 512, 512], P('sec', None, None, 'pan'), may hold values from -0.25 to 0.25
- left_blocks: bfloat16 [576, 512, 512], P('sec', 'pan'), may hold values from -0.125 to 0.125
- coupling: bfloat16 [576], P('sec'), may hold values from -1 to 1
- channel_term: int32 [576], P('sec'), may hold values from 0 to 15
- channel_out: int32 [576], P('sec'), may hold values from 0 to 7, as said below
- sector_dims: int32 [8], P('sec'), may hold values from 128 to 512
Outputs:
- applied: float32 [8, 512, 512], P('sec', 'pan')
Inputs may be any that keep to these rules, and one draw needn't show every extreme that they name: `channel_out`: channel c ends in a sector at most two away from the sector c // 72 that it starts from.
All inputs are finite; a program needn't handle non-finite values.
Results may differ from a plain program's by a relative error of at most 0.0041.
Values may be sent and summed in bfloat16 or wider, within the bound.
A program may use at most 128 MiB of HBM per device.

v0:
```python
import functools

import jax
import jax.numpy as jnp
from jax import lax
from jax.experimental import pallas as pl
from jax.experimental.pallas import tpu as pltpu
from jax.sharding import PartitionSpec as P

OFFSETS = (-2, -1, 1, 2)
F32 = jnp.float32
BF16 = jnp.bfloat16


def combine_kernel(cell_ref, coef_ref, left_ref, out_ref, acc_ref):
    acc_ref[...] = jnp.zeros_like(acc_ref)

    @pl.loop(0, left_ref.shape[0])
    def _(channel):
        cell = cell_ref[channel]
        acc_ref[cell] += left_ref[channel].astype(F32) * coef_ref[channel]

    @pl.loop(0, out_ref.shape[0])
    def _(cell):
        out_ref[cell] = acc_ref[cell].astype(BF16)


def combine(cells, coefs, left_blocks, cell_count):
    channels, rows, width = left_blocks.shape
    step = min(rows, 32)
    return pl.pallas_call(
        combine_kernel,
        grid=(rows // step,),
        in_specs=[
            pl.BlockSpec(memory_space=pltpu.SMEM),
            pl.BlockSpec(memory_space=pltpu.SMEM),
            pl.BlockSpec((channels, step, width), lambda i: (0, i, 0)),
        ],
        out_specs=pl.BlockSpec((cell_count, step, width), lambda i: (0, i, 0)),
        out_shape=jax.ShapeDtypeStruct((cell_count, rows, width), BF16),
        scratch_shapes=[pltpu.VMEM((cell_count, step, width), F32)],
        compiler_params=pltpu.CompilerParams(vmem_limit_bytes=48 * 2**20),
    )(cells, coefs, left_blocks)


def order_kernel(slots, term_ref, out_ids_ref, coef_ref, table_ref, sorted_ref, spots):
    channels = term_ref.shape[0]
    cells = spots.shape[0]
    last_at, filled_at = 2 * channels, 2 * channels + cells
    sector = lax.axis_index("sec")

    def cell_of(channel):
        return term_ref[channel] * slots + out_ids_ref[channel] - sector + 2

    @pl.loop(0, cells)
    def _(cell):
        spots[cell] = 0

    @pl.loop(0, channels)
    def _(channel):
        spots[cell_of(channel)] += 1

    def lay_out(cell, start):
        count = spots[cell]
        spots[cell] = start
        table_ref[last_at + cell] = jnp.maximum(start + count - 1, 0)
        table_ref[filled_at + cell] = jnp.minimum(count, 1)
        return start + count

    lax.fori_loop(0, cells, lay_out, 0)

    @pl.loop(0, channels)
    def _(channel):
        table_ref[channels + channel] = 1

    @pl.loop(0, cells)
    def _(cell):
        table_ref[channels + jnp.minimum(spots[cell], channels - 1)] = jnp.where(
            table_ref[filled_at + cell] > 0,
            0,
            table_ref[channels + jnp.minimum(spots[cell], channels - 1)],
        )

    @pl.loop(0, channels)
    def _(channel):
        cell = cell_of(channel)
        spot = spots[cell]
        spots[cell] = spot + 1
        table_ref[spot] = channel
        sorted_ref[spot] = coef_ref[channel]


def order_channels(slots, cells, channel_term, channel_out, coefs):
    channels = coefs.shape[0]
    smem = pl.BlockSpec(memory_space=pltpu.SMEM)
    return pl.pallas_call(
        functools.partial(order_kernel, slots),
        out_shape=(
            jax.ShapeDtypeStruct((2 * channels + 2 * cells,), jnp.int32),
            jax.ShapeDtypeStruct((channels,), F32),
        ),
        in_specs=[smem] * 3,
        out_specs=(smem, smem),
        scratch_shapes=[pltpu.SMEM((cells,), jnp.int32)],
    )(channel_term, channel_out, coefs)


def line_kernel(
    sectors, moved, dims_ref, table_ref, coef_ref, state_ref, right_ref, left_ref, out_ref,
    left_all, running, summed,
    state_all, masked, gathered, comb, comb_end, acc, acc_end,
    stage, landed, stage_end, landed_end, back, back_landed,
    local_sems, state_send, state_recv, own_send, relay_send, right_recv,
    end_send, end_recv, part_send, part_recv, part_end_send, part_end_recv, back_sems,
):
    terms, width, cols = right_ref.shape
    rows = state_ref.shape[0]
    slots = comb.shape[1] // rows
    me = lax.axis_index("pan")
    sector = lax.axis_index("sec")
    is_mid = (me == 1) | (me == 2)
    is_end = jnp.logical_not(is_mid)
    near_end = jnp.where(me <= 1, 0, 3)
    other_mid = jnp.where(me <= 1, 2, 1)
    far_end = 3 - near_end
    near_mid = jnp.where(me <= 1, 1, 2)

    def remote(src, dst, send, recv, where, axis="pan"):
        return pltpu.make_async_remote_copy(
            src_ref=src, dst_ref=dst, send_sem=send, recv_sem=recv,
            device_id={axis: where}, device_id_type=pl.DeviceIdType.MESH,
        )

    def state_copy(shift):
        where = lax.rem(me + shift, 4)
        spot = state_all.at[me]
        return remote(state_ref, spot, state_send.at[shift], state_recv.at[me], where)

    def state_wait(owner):
        remote(state_ref, state_all.at[owner], state_send.at[0], state_recv.at[owner], me).wait_recv()

    def own_copy(way, term, where):
        return remote(
            right_ref.at[term], gathered.at[me, term],
            own_send.at[way, term], right_recv.at[me, term], where,
        )

    def relay_copy(way, owner, term, where):
        block = gathered.at[owner, term]
        return remote(block, block, relay_send.at[way, term], right_recv.at[owner, term], where)

    def end_copy(term):
        return remote(comb.at[term], comb_end.at[term], end_send.at[term], end_recv.at[term], near_mid)

    def arrived(owner, term):
        block = gathered.at[owner, term]
        remote(block, block, relay_send.at[0, term], right_recv.at[owner, term], me).wait_recv()

    def part_copy(index, owner):
        return remote(
            stage.at[index, owner], landed.at[index, owner],
            part_send.at[index, owner], part_recv.at[index, owner], sector + OFFSETS[index], "sec",
        )

    def part_end_copy(index):
        return remote(
            stage_end.at[index], landed_end.at[index],
            part_end_send.at[index], part_end_recv.at[index], sector + OFFSETS[index], "sec",
        )

    def goes(index):
        target = sector + OFFSETS[index]
        return (target >= 0) & (target < sectors)

    def comes(index):
        source = sector - OFFSETS[index]
        return (source >= 0) & (source < sectors)

    for shift in (1, 2, 3):
        state_copy(shift).start()

    @pl.when(is_mid)
    def _():
        @pl.loop(0, terms)
        def _(term):
            own_copy(0, term, other_mid).start()

            @pl.when(term >= moved)
            def _():
                own_copy(1, term, near_end).start()

    @pl.when(is_end)
    def _():
        @pl.loop(0, terms)
        def _(term):
            own_copy(0, term, near_mid).start()

    copies = [
        pltpu.make_async_copy(state_ref, state_all.at[me], local_sems.at[0]),
        pltpu.make_async_copy(right_ref, gathered.at[me], local_sems.at[1]),
        pltpu.make_async_copy(left_ref, left_all, local_sems.at[2]),
    ]
    for copy in copies:
        copy.start()
    acc[...] = jnp.zeros_like(acc)
    acc_end[...] = jnp.zeros_like(acc_end)
    running[...] = jnp.zeros_like(running)
    for copy in copies:
        copy.wait()

    channels = left_all.shape[0]
    cells = terms * slots

    @pl.loop(0, channels)
    def _(step):
        kept = table_ref[channels + step].astype(F32)
        total = running[...] * kept + left_all[table_ref[step]].astype(F32) * coef_ref[step]
        running[...] = total
        summed[step] = total.astype(BF16)

    @pl.loop(0, terms)
    def _(term):
        for slot in range(slots):
            cell = term * slots + slot
            filled = table_ref[2 * channels + cells + cell].astype(F32)
            value = summed[table_ref[2 * channels + cell]].astype(F32) * filled
            comb[term, slot * rows:(slot + 1) * rows, :] = value.astype(BF16)

    for shift in (1, 2, 3):
        state_wait(lax.rem(me + shift, 4))

    @pl.when(is_end)
    def _():
        @pl.loop(0, moved)
        def _(term):
            end_copy(term).start()

    live = dims_ref[0]
    inside_col = lax.broadcasted_iota(jnp.int32, (rows, width), 1) < live
    for owner in range(4):
        row = lax.broadcasted_iota(jnp.int32, (rows, width), 0) + owner * rows
        masked[owner * rows:(owner + 1) * rows, :] = jnp.where(
            inside_col & (row < live), state_all[owner].astype(F32), 0.0
        ).astype(BF16)

    def multiply(owner, term, left, total):
        block = jnp.dot(masked[...], gathered[owner, term], preferred_element_type=F32).astype(BF16)
        total[owner] += jnp.dot(left[term], block, preferred_element_type=F32)

    def send_parts(owner):
        for index in range(4):
            slot = OFFSETS[index] + 2

            @pl.when(goes(index))
            def _():
                stage[index, owner] = acc[owner, slot * rows:(slot + 1) * rows, :].astype(BF16)
                part_copy(index, owner).start()

    @pl.when(is_mid)
    def _():
        @pl.loop(0, terms)
        def _(term):
            arrived(other_mid, term)

            @pl.when(term >= moved)
            def _():
                relay_copy(0, other_mid, term, near_end).start()

            arrived(near_end, term)
            relay_copy(1, near_end, term, other_mid).start()

            @pl.loop(0, 3)
            def _(which):
                owner = jnp.where(which == 0, me, jnp.where(which == 1, other_mid, near_end))
                multiply(owner, term, comb, acc)

        @pl.loop(0, 3)
        def _(which):
            send_parts(jnp.where(which == 0, me, jnp.where(which == 1, other_mid, near_end)))

        @pl.loop(0, terms)
        def _(term):
            arrived(far_end, term)

            @pl.when(term >= moved)
            def _():
                relay_copy(2, far_end, term, near_end).start()

            multiply(far_end, term, comb, acc)

        send_parts(far_end)

        @pl.loop(0, moved)
        def _(term):
            remote(comb.at[term], comb_end.at[term], end_send.at[term], end_recv.at[term], me).wait_recv()

            @pl.loop(0, 4)
            def _(owner):
                multiply(owner, term, comb_end, acc_end)

        for index in range(4):
            slot = OFFSETS[index] + 2

            @pl.when(goes(index))
            def _():
                stage_end[index] = acc_end[:, slot * rows:(slot + 1) * rows, :].astype(BF16)
                part_end_copy(index).start()

        for index in range(4):
            @pl.when(comes(index))
            def _():
                part_end_copy(index).wait_recv()
                acc_end[:, 2 * rows:3 * rows, :] += landed_end[index].astype(F32)

        back[...] = acc_end[:, 2 * rows:3 * rows, :].astype(BF16)
        remote(back, back_landed, back_sems.at[0], back_sems.at[1], near_end).start()

    @pl.when(is_end)
    def _():
        turn = jnp.where(me == 0, 1, -1)

        @pl.loop(0, 4)
        def _(rank):
            owner = me + turn * rank

            @pl.loop(moved, terms)
            def _(term):
                @pl.when(rank > 0)
                def _():
                    arrived(owner, term)

                multiply(owner, term, comb, acc)

            send_parts(owner)

    for index in range(4):
        @pl.when(comes(index))
        def _():
            @pl.loop(0, 4)
            def _(owner):
                part_copy(index, owner).wait_recv()
                acc[owner, 2 * rows:3 * rows, :] += landed[index, owner].astype(F32)

    @pl.when(is_end)
    def _():
        remote(back, back_landed, back_sems.at[0], back_sems.at[1], me).wait_recv()
        acc[:, 2 * rows:3 * rows, :] += back_landed[...].astype(F32)

    for owner in range(4):
        out_ref[:, owner * cols:(owner + 1) * cols] = acc[owner, 2 * rows:3 * rows, :]

    for shift in (1, 2, 3):
        state_copy(shift).wait_send()
    for index in range(4):
        @pl.when(goes(index))
        def _():
            @pl.loop(0, 4)
            def _(owner):
                part_copy(index, owner).wait_send()

            @pl.when(is_mid)
            def _():
                part_end_copy(index).wait_send()

    @pl.when(is_mid)
    def _():
        @pl.loop(0, terms)
        def _(term):
            own_copy(0, term, other_mid).wait_send()
            relay_copy(1, near_end, term, other_mid).wait_send()

            @pl.when(term >= moved)
            def _():
                own_copy(1, term, near_end).wait_send()
                relay_copy(0, other_mid, term, near_end).wait_send()
                relay_copy(2, far_end, term, near_end).wait_send()

        remote(back, back_landed, back_sems.at[0], back_sems.at[1], near_end).wait_send()

    @pl.when(is_end)
    def _():
        @pl.loop(0, terms)
        def _(term):
            own_copy(0, term, near_mid).wait_send()

        @pl.loop(0, moved)
        def _(term):
            end_copy(term).wait_send()


def line_apply(sectors, slots, dims, table, coefs, state, right, left):
    terms, width, cols = right.shape
    rows = state.shape[0]
    moved = max(1, (terms * 3) // 16)
    tall = slots * rows
    dma = pltpu.SemaphoreType.DMA
    any_space = pl.BlockSpec(memory_space=pl.ANY)
    return pl.pallas_call(
        functools.partial(line_kernel, sectors, moved),
        out_shape=jax.ShapeDtypeStruct((rows, width), F32),
        in_specs=[pl.BlockSpec(memory_space=pltpu.SMEM)] * 3 + [any_space] * 3,
        out_specs=pl.BlockSpec(memory_space=pltpu.VMEM),
        scratch_shapes=[
            pltpu.VMEM(left.shape, BF16),
            pltpu.VMEM((rows, width), F32),
            pltpu.VMEM(left.shape, BF16),
            pltpu.VMEM((4, rows, width), BF16),
            pltpu.VMEM((width, width), BF16),
            pltpu.VMEM((4, terms, width, cols), BF16),
            pltpu.VMEM((terms, tall, width), BF16),
            pltpu.VMEM((moved, tall, width), BF16),
            pltpu.VMEM((4, tall, cols), F32),
            pltpu.VMEM((4, tall, cols), F32),
            pltpu.VMEM((4, 4, rows, cols), BF16),
            pltpu.VMEM((4, 4, rows, cols), BF16),
            pltpu.VMEM((4, 4, rows, cols), BF16),
            pltpu.VMEM((4, 4, rows, cols), BF16),
            pltpu.VMEM((4, rows, cols), BF16),
            pltpu.VMEM((4, rows, cols), BF16),
            dma((3,)), dma((4,)), dma((4,)),
            dma((2, terms)), dma((3, terms)), dma((4, terms)),
            dma((moved,)), dma((moved,)),
            dma((4, 4)), dma((4, 4)), dma((4,)), dma((4,)), dma((2,)),
        ],
        compiler_params=pltpu.CompilerParams(
            has_side_effects=True, vmem_limit_bytes=56 * 2**20
        ),
    )(dims, table, coefs, state, right, left)


def passed_along(value, axis, steps):
    count = lax.axis_size(axis)
    first, last = (max(0, -steps), min(count, count - steps))
    return lax.ppermute(value, axis, [(source, source + steps) for source in range(first, last)])


def gathered_apply(sector, live_dim, wave, right, combined, rows, slots):
    width = wave.shape[1]
    terms = right.shape[0]
    whole_state = lax.all_gather(wave, "pan", axis=0, tiled=True)
    indices = lax.iota(jnp.int32, width)
    inside = (indices[:, None] < live_dim) & (indices[None, :] < live_dim)
    masked = jnp.where(inside, whole_state, jnp.zeros((), BF16))
    right_full = lax.all_gather(right, "pan", axis=2, tiled=True)
    term_full = jnp.einsum("ik,wkq->wiq", masked, right_full, preferred_element_type=F32).astype(BF16)
    parts = jnp.einsum(
        "wjri,wiq->jrq", combined.reshape(terms, slots, rows, width), term_full,
        preferred_element_type=F32,
    )
    collected = parts[2]
    for offset in OFFSETS:
        collected = collected + passed_along(parts[offset + 2], "sec", offset)
    return collected


def on_device(
    wave_state, right_blocks, left_blocks, coupling, channel_term, channel_out, sector_dims
):
    rows, width = wave_state.shape[1:]
    terms = right_blocks.shape[1]
    slots = 5
    sector = lax.axis_index("sec")
    live_dim = sector_dims[0]
    cells = channel_term * slots + channel_out - sector + 2
    coefs = coupling.astype(F32)
    if lax.axis_size("pan") == 4 and right_blocks.shape[3] % 128 == 0:
        table, ordered = order_channels(slots, terms * slots, channel_term, channel_out, coefs)
        collected = line_apply(
            lax.axis_size("sec"), slots, sector_dims, table, ordered,
            wave_state[0], right_blocks[0], left_blocks,
        )
    else:
        combined = combine(cells, coefs, left_blocks, terms * slots)
        collected = gathered_apply(
            sector, live_dim, wave_state[0], right_blocks[0], combined, rows, slots
        )
    indices = lax.iota(jnp.int32, width)
    row_ids = lax.axis_index("pan") * rows + lax.iota(jnp.int32, rows)
    kept_mask = (row_ids[:, None] < live_dim) & (indices[None, :] < live_dim)
    return jnp.where(kept_mask, collected, jnp.zeros((), F32))[None]


def solution(mesh):
    return jax.shard_map(
        on_device,
        mesh=mesh,
        in_specs=(
            P("sec", "pan", None),
            P("sec", None, None, "pan"),
            P("sec", "pan", None),
            P("sec"),
            P("sec"),
            P("sec"),
            P("sec"),
        ),
        out_specs=P("sec", "pan", None),
        check_vma=False,
    )
```

profile of v0, /device:TPU:0, one launch (start us, length us, event | category | flops | bytes accessed | tf_op | source)
XLA Modules:
  0.0 144.9 jit_solution(12505389195447245324)
XLA Ops:
  0.7 1.2 convert_element_type.3.coef_ref
  1.8 5.5 %shard_map.73 = (s32[304]{0:T(512)}, f32[72]{0:T(128)}) custom-call(s32[72]{0:T(128)} %term_ref.1, s32[72]{0:T(128)} %out_ids_ref.1, f32[72]{0:T(128)} %convert_element_type.3.coef_ref), custom_call_target="tpu_custom_call" | custom-call | tf_op jit(solution)/shard_map/pallas_call | solution.py:96
  7.3 135.9 %shard_map.74 = f32[128,512]{1,0:T(8,128)} custom-call(s32[1]{0:T(128)} %copy.8.dims_ref, s32[304]{0:T(512)} %get-tuple-element.7.table_ref, f32[72]{0:T(128)} %get-tuple-element.8.coef_ref, bf16[128,512]{1,0:T(8,128)(2,1)} %bitcast.8, bf16[16,512,128]{2,1,0:T(8,128)(2,1)} %bitcast.7, bf16[72,128,512]{2,1,0:T(8,128)(2,1)} %left_ref.1), custom_call_target="tpu_custom_call" | custom-call | tf_op jit(solution)/shard_map/pallas_call | solution.py:398
  143.2 1.8 %select_bitcast_fusion = f32[1,128,512]{2,1,0:T(8,128)} fusion(f32[128,512]{1,0:T(8,128)} %shard_map.74, pred[512]{0:T(512)(128)(4,1)S(1)} %iota_compare_fusion, pred[128]{0:T(512)(128)(4,1)S(1)} %add_compare_fusion), kind=kLoop, calls=%fused_computation | loop fusion | flops 131072 | bytes 524928 | tf_op jit(solution)/shard_map/broadcast_in_dim | solution.py:480
  (2 shorter events, 0.0 us)
where the time goes:
time: 147 us; the launch traced here: 145 us
  Pallas kernels  141 us (96%)
  other arithmetic  2.92 us (2%)
    pallas_call x1, Pallas kernels, line_apply(): pl.pallas_call(functools.partial(line_kernel, sectors, moved), out_shape=...  136 us
    pallas_call x1, Pallas kernels, order_channels(): pl.pallas_call(functools.partial(order_kernel, slots), out_shape=(jax.Sha...  5.46 us

commit v1 on v0

v1 whole, which is shorter than its diff:
```python
import functools

import jax
import jax.numpy as jnp
from jax import lax
from jax.experimental import pallas as pl
from jax.experimental.pallas import tpu as pltpu
from jax.sharding import PartitionSpec as P

OFFSETS = (-2, -1, 1, 2)
END_SLOTS = (0, 1, 3, 4, 2)
F32 = jnp.float32
BF16 = jnp.bfloat16


def combine_kernel(cell_ref, coef_ref, left_ref, out_ref, acc_ref):
    acc_ref[...] = jnp.zeros_like(acc_ref)

    @pl.loop(0, left_ref.shape[0])
    def _(channel):
        cell = cell_ref[channel]
        acc_ref[cell] += left_ref[channel].astype(F32) * coef_ref[channel]

    @pl.loop(0, out_ref.shape[0])
    def _(cell):
        out_ref[cell] = acc_ref[cell].astype(BF16)


def combine(cells, coefs, left_blocks, cell_count):
    channels, rows, width = left_blocks.shape
    step = min(rows, 32)
    return pl.pallas_call(
        combine_kernel,
        grid=(rows // step,),
        in_specs=[
            pl.BlockSpec(memory_space=pltpu.SMEM),
            pl.BlockSpec(memory_space=pltpu.SMEM),
            pl.BlockSpec((channels, step, width), lambda i: (0, i, 0)),
        ],
        out_specs=pl.BlockSpec((cell_count, step, width), lambda i: (0, i, 0)),
        out_shape=jax.ShapeDtypeStruct((cell_count, rows, width), BF16),
        scratch_shapes=[pltpu.VMEM((cell_count, step, width), F32)],
        compiler_params=pltpu.CompilerParams(vmem_limit_bytes=48 * 2**20),
    )(cells, coefs, left_blocks)


def read_channels(slots, terms, sector, term, out_id, coef, coefs, kept, filled, table):
    count = term.shape[0]
    cells = slots * terms
    width = coefs.shape[1]
    cell = (term[...] * slots + out_id[...] - sector + 2).astype(F32)
    cell_row = jnp.broadcast_to(cell[None, :], (count, count))
    coef_row = jnp.broadcast_to(coef[...].astype(F32)[None, :], (count, count))
    down = lax.broadcasted_iota(jnp.int32, (count, count), 0)
    across = lax.broadcasted_iota(jnp.int32, (count, count), 1)

    def total(mask, values, axis):
        return jnp.sum(jnp.where(mask, values, 0.0), axis=axis, keepdims=True)

    cell_col = total(down == across, cell_row, 1)
    same = cell_col == cell_row
    precedes = (cell_col < cell_row) | (same & (down < across))
    follows = (cell_row < cell_col) | (same & (across < down))
    rank_row = total(precedes, 1.0, 0)
    rank_col = total(follows, 1.0, 1)
    again = jnp.where(total(same & (down < across), 1.0, 0) > 0, 1.0, 0.0)
    spot = rank_row == down.astype(F32)
    coefs[...] = jnp.broadcast_to(total(spot, coef_row, 1), (count, width))
    kept[...] = jnp.broadcast_to(
        total(spot, jnp.broadcast_to(again, (count, count)), 1), (count, width)
    )
    order = total(rank_col == across.astype(F32), down.astype(F32), 0)
    cell_ids = lax.broadcasted_iota(jnp.int32, (count, cells), 1).astype(F32)
    last = total(jnp.broadcast_to(cell_col, (count, cells)) <= cell_ids, 1.0, 0) - 1.0
    ids_down = lax.broadcasted_iota(jnp.int32, (cells, count), 0).astype(F32)
    held = total(ids_down == jnp.broadcast_to(cell[None, :], (cells, count)), 1.0, 1)
    filled[...] = jnp.broadcast_to(jnp.where(held > 0, 1.0, 0.0), (cells, width))
    table[0:1, 0:count] = order.astype(jnp.int32)
    table[1:2, 0:cells] = jnp.maximum(last, 0.0).astype(jnp.int32)


def line_kernel(
    sectors, moved, dims_ref, term_ref, out_id_ref, coef_ref, state_ref, right_ref, left_ref,
    out_ref,
    dims, term_ids, out_ids, coef, table, spots, coefs, kept, filled,
    left_all, running, summed,
    state_all, masked, gathered, comb, comb_end, kept_terms, acc, acc_end,
    stage, landed, stage_end, landed_end, back, back_landed,
    local_sems, state_send, state_recv, own_send, relay_send, right_recv,
    end_send, end_recv, part_send, part_recv, part_end_send, part_end_recv, back_sems,
):
    terms, width, cols = right_ref.shape
    rows = state_ref.shape[0]
    slots = comb.shape[1] // rows
    home = slots // 2
    me = lax.axis_index("pan")
    sector = lax.axis_index("sec")
    is_mid = (me == 1) | (me == 2)
    is_end = jnp.logical_not(is_mid)
    near_end = jnp.where(me <= 1, 0, 3)
    other_mid = jnp.where(me <= 1, 2, 1)
    far_end = 3 - near_end
    near_mid = jnp.where(me <= 1, 1, 2)

    def remote(src, dst, send, recv, where, axis="pan"):
        return pltpu.make_async_remote_copy(
            src_ref=src, dst_ref=dst, send_sem=send, recv_sem=recv,
            device_id={axis: where}, device_id_type=pl.DeviceIdType.MESH,
        )

    def state_own(way, where):
        return remote(state_ref, state_all.at[me], state_send.at[way], state_recv.at[me], where)

    def state_relay(way, owner, where):
        block = state_all.at[owner]
        return remote(block, block, state_send.at[way], state_recv.at[owner], where)

    def state_wait(owner):
        state_relay(0, owner, me).wait_recv()

    def own_copy(way, term, where):
        return remote(
            right_ref.at[term], gathered.at[me, term],
            own_send.at[way, term], right_recv.at[me, term], where,
        )

    def relay_copy(way, owner, term, where):
        block = gathered.at[owner, term]
        return remote(block, block, relay_send.at[way, term], right_recv.at[owner, term], where)

    def end_copy(slot, term, where):
        spot = pl.ds(pl.multiple_of(slot * rows, rows), rows)
        return remote(
            comb.at[term, spot], comb_end.at[slot, term],
            end_send.at[slot, term], end_recv.at[slot, term], where,
        )

    def arrived(owner, term):
        block = gathered.at[owner, term]
        remote(block, block, relay_send.at[0, term], right_recv.at[owner, term], me).wait_recv()

    def part_copy(index, owner):
        return remote(
            stage.at[index, owner], landed.at[index, owner],
            part_send.at[index, owner], part_recv.at[index, owner], sector + OFFSETS[index], "sec",
        )

    def part_end_copy(index):
        return remote(
            stage_end.at[index], landed_end.at[index],
            part_end_send.at[index], part_end_recv.at[index], sector + OFFSETS[index], "sec",
        )

    def back_copy(where):
        return remote(back, back_landed, back_sems.at[0], back_sems.at[1], where)

    def goes(index):
        target = sector + OFFSETS[index]
        return (target >= 0) & (target < sectors)

    def comes(index):
        source = sector - OFFSETS[index]
        return (source >= 0) & (source < sectors)

    barrier = pltpu.get_barrier_semaphore()

    def greet(axis, where):
        pl.semaphore_signal(
            barrier, inc=1, device_id={axis: where}, device_id_type=pl.DeviceIdType.MESH
        )

    greet("pan", jnp.where(is_mid, near_end, near_mid))

    @pl.when(is_mid)
    def _():
        greet("pan", other_mid)

    peers = jnp.where(is_mid, 2, 1)
    for index in range(4):
        peers = peers + goes(index).astype(jnp.int32)

        @pl.when(goes(index))
        def _():
            greet("sec", sector + OFFSETS[index])

    pl.semaphore_wait(barrier, peers)

    early = min(2, terms - moved)

    @pl.when(is_mid)
    def _():
        state_own(0, near_end).start()
        state_own(1, other_mid).start()

        @pl.loop(0, early)
        def _(term):
            own_copy(1, moved + term, near_end).start()
            own_copy(0, term, other_mid).start()

    @pl.when(is_end)
    def _():
        state_own(0, near_mid).start()

        @pl.loop(0, terms)
        def _(term):
            own_copy(0, term, near_mid).start()

    small = [
        pltpu.make_async_copy(dims_ref, dims, local_sems.at[0]),
        pltpu.make_async_copy(term_ref, term_ids, local_sems.at[1]),
        pltpu.make_async_copy(out_id_ref, out_ids, local_sems.at[2]),
        pltpu.make_async_copy(coef_ref, coef, local_sems.at[3]),
    ]
    large = [
        pltpu.make_async_copy(left_ref, left_all, local_sems.at[4]),
        pltpu.make_async_copy(state_ref, state_all.at[me], local_sems.at[5]),
        pltpu.make_async_copy(right_ref, gathered.at[me], local_sems.at[6]),
    ]
    for copy in small + large:
        copy.start()
    for copy in small:
        copy.wait()
    read_channels(slots, terms, sector, term_ids, out_ids, coef, coefs, kept, filled, table)
    spots_copy = pltpu.make_async_copy(table, spots, local_sems.at[7])
    spots_copy.start()
    acc[...] = jnp.zeros_like(acc)
    acc_end[...] = jnp.zeros_like(acc_end)
    running[...] = jnp.zeros_like(running)

    later = min(early + 3, terms - moved)

    @pl.when(is_mid)
    def _():
        state_wait(other_mid)
        state_relay(2, other_mid, near_end).start()
        state_wait(near_end)
        state_relay(3, near_end, other_mid).start()

        @pl.loop(early, later)
        def _(term):
            own_copy(1, moved + term, near_end).start()

        @pl.loop(early, terms)
        def _(term):
            own_copy(0, term, other_mid).start()

    spots_copy.wait()
    for copy in large:
        copy.wait()

    channels = left_all.shape[0]

    def inside(spot):
        return jnp.minimum(jnp.maximum(spot, 0), channels - 1)

    @pl.loop(0, channels)
    def _(step):
        row = pl.ds(step, 1)
        total = running[...] * kept[row, :] + left_all[inside(spots[0, step])].astype(F32) * coefs[row, :]
        running[...] = total
        summed[step] = total.astype(BF16)

    @pl.loop(0, terms)
    def _(term):
        for slot in range(slots):
            cell = term * slots + slot
            value = summed[inside(spots[1, cell])].astype(F32) * filled[pl.ds(cell, 1), :]
            comb[term, slot * rows:(slot + 1) * rows, :] = value.astype(BF16)

    @pl.when(is_mid)
    def _():
        state_wait(far_end)
        state_relay(4, far_end, near_end).start()

        @pl.loop(later, terms - moved)
        def _(term):
            own_copy(1, moved + term, near_end).start()

    @pl.when(is_end)
    def _():
        for slot in END_SLOTS:
            @pl.loop(0, moved)
            def _(term):
                end_copy(slot, term, near_mid).start()

        for owner in (near_mid, 3 - near_mid, 3 - me):
            state_wait(owner)

    live = dims[0]
    inside_col = lax.broadcasted_iota(jnp.int32, (rows, width), 1) < live
    for owner in range(4):
        row = lax.broadcasted_iota(jnp.int32, (rows, width), 0) + owner * rows
        masked[owner * rows:(owner + 1) * rows, :] = jnp.where(
            inside_col & (row < live), state_all[owner].astype(F32), 0.0
        ).astype(BF16)

    def multiply(owner, term, keep=False):
        block = jnp.dot(masked[...], gathered[owner, term], preferred_element_type=F32).astype(BF16)
        if keep:
            kept_terms[term, owner] = block
        acc[owner] += jnp.dot(comb[term], block, preferred_element_type=F32)

    def send_parts(owner):
        for index in range(4):
            slot = OFFSETS[index] + 2

            @pl.when(goes(index))
            def _():
                stage[index, owner] = acc[owner, slot * rows:(slot + 1) * rows, :].astype(BF16)
                part_copy(index, owner).start()

    def take_parts(owner):
        for index in range(4):
            @pl.when(comes(index))
            def _():
                part_copy(index, owner).wait_recv()
                acc[owner, home * rows:(home + 1) * rows, :] += landed[index, owner].astype(F32)

    def write_out(owner):
        for spot in range(4):
            @pl.when(owner == spot)
            def _():
                out_ref[:, spot * cols:(spot + 1) * cols] = acc[spot, home * rows:(home + 1) * rows, :]

    def end_slot(slot):
        @pl.loop(0, moved)
        def _(term):
            end_copy(slot, term, me).wait_recv()

            @pl.loop(0, 4)
            def _(owner):
                acc_end[slot, owner] += jnp.dot(
                    comb_end[slot, term], kept_terms[term, owner], preferred_element_type=F32
                )

    @pl.when(is_mid)
    def _():
        def first_pass(begin, end, keep):
            @pl.loop(begin, end)
            def _(term):
                arrived(other_mid, term)
                if not keep:
                    relay_copy(0, other_mid, term, near_end).start()
                arrived(near_end, term)
                relay_copy(1, near_end, term, other_mid).start()

                @pl.loop(0, 3)
                def _(which):
                    owner = jnp.where(which == 0, me, jnp.where(which == 1, other_mid, near_end))
                    multiply(owner, term, keep)

        first_pass(0, moved, True)
        first_pass(moved, terms, False)

        @pl.loop(0, 3)
        def _(which):
            send_parts(jnp.where(which == 0, me, jnp.where(which == 1, other_mid, near_end)))

        @pl.loop(0, moved)
        def _(term):
            arrived(far_end, term)
            multiply(far_end, term, True)

        @pl.loop(moved, terms)
        def _(term):
            arrived(far_end, term)
            relay_copy(2, far_end, term, near_end).start()
            multiply(far_end, term)

            for index in range(4):
                slot = OFFSETS[index] + 2

                @pl.when(term == turn_of(index, moved, terms))
                def _():
                    end_slot(slot)

                    @pl.when(goes(index))
                    def _():
                        stage_end[index] = acc_end[slot].astype(BF16)
                        part_end_copy(index).start()

        send_parts(far_end)
        end_slot(home)

        for index in range(4):
            @pl.when(comes(index))
            def _():
                part_end_copy(index).wait_recv()
                acc_end[home] += landed_end[index].astype(F32)

        back[...] = acc_end[home].astype(BF16)
        back_copy(near_end).start()

        @pl.loop(0, 4)
        def _(owner):
            take_parts(owner)
            write_out(owner)

    @pl.when(is_end)
    def _():
        turn = jnp.where(me == 0, 1, -1)

        @pl.loop(0, 4)
        def _(rank):
            owner = me + turn * rank

            @pl.loop(moved, terms)
            def _(term):
                @pl.when(rank > 0)
                def _():
                    arrived(owner, term)

                multiply(owner, term)

            send_parts(owner)

        @pl.loop(0, 4)
        def _(rank):
            take_parts(me + turn * rank)

        back_copy(me).wait_recv()
        acc[:, home * rows:(home + 1) * rows, :] += back_landed[...].astype(F32)

        @pl.loop(0, 4)
        def _(owner):
            write_out(owner)

    for index in range(4):
        @pl.when(goes(index))
        def _():
            @pl.loop(0, 4)
            def _(owner):
                part_copy(index, owner).wait_send()

            @pl.when(is_mid)
            def _():
                part_end_copy(index).wait_send()

    @pl.when(is_mid)
    def _():
        state_own(0, near_end).wait_send()
        state_own(1, other_mid).wait_send()
        state_relay(2, other_mid, near_end).wait_send()
        state_relay(3, near_end, other_mid).wait_send()
        state_relay(4, far_end, near_end).wait_send()

        @pl.loop(0, terms)
        def _(term):
            own_copy(0, term, other_mid).wait_send()
            relay_copy(1, near_end, term, other_mid).wait_send()

            @pl.when(term >= moved)
            def _():
                own_copy(1, term, near_end).wait_send()
                relay_copy(0, other_mid, term, near_end).wait_send()
                relay_copy(2, far_end, term, near_end).wait_send()

        back_copy(near_end).wait_send()

    @pl.when(is_end)
    def _():
        state_own(0, near_mid).wait_send()

        @pl.loop(0, terms)
        def _(term):
            own_copy(0, term, near_mid).wait_send()

        for slot in END_SLOTS:
            @pl.loop(0, moved)
            def _(term):
                end_copy(slot, term, near_mid).wait_send()


def turn_of(index, moved, terms):
    steps = terms - moved
    return moved + min(steps - 1, max(0, (steps * (4 * index - 2)) // 12))


def line_apply(sectors, slots, dims, channel_term, channel_out, coefs, state, right, left):
    terms, width, cols = right.shape
    rows = state.shape[0]
    channels = left.shape[0]
    cells = slots * terms
    moved = max(1, terms // 4)
    tall = slots * rows
    dma = pltpu.SemaphoreType.DMA
    any_space = pl.BlockSpec(memory_space=pl.ANY)
    return pl.pallas_call(
        functools.partial(line_kernel, sectors, moved),
        out_shape=jax.ShapeDtypeStruct((rows, width), F32),
        in_specs=[any_space] * 7,
        out_specs=pl.BlockSpec(memory_space=pltpu.VMEM),
        scratch_shapes=[
            pltpu.SMEM(dims.shape, jnp.int32),
            pltpu.VMEM((channels,), jnp.int32),
            pltpu.VMEM((channels,), jnp.int32),
            pltpu.VMEM((channels,), BF16),
            pltpu.VMEM((8, 128), jnp.int32),
            pltpu.SMEM((8, 128), jnp.int32),
            pltpu.VMEM((channels, width), F32),
            pltpu.VMEM((channels, width), F32),
            pltpu.VMEM((cells, width), F32),
            pltpu.VMEM(left.shape, BF16),
            pltpu.VMEM((rows, width), F32),
            pltpu.VMEM(left.shape, BF16),
            pltpu.VMEM((4, rows, width), BF16),
            pltpu.VMEM((width, width), BF16),
            pltpu.VMEM((4, terms, width, cols), BF16),
            pltpu.VMEM((terms, tall, width), BF16),
            pltpu.VMEM((slots, moved, rows, width), BF16),
            pltpu.VMEM((moved, 4, width, cols), BF16),
            pltpu.VMEM((4, tall, cols), F32),
            pltpu.VMEM((slots, 4, rows, cols), F32),
            pltpu.VMEM((4, 4, rows, cols), BF16),
            pltpu.VMEM((4, 4, rows, cols), BF16),
            pltpu.VMEM((4, 4, rows, cols), BF16),
            pltpu.VMEM((4, 4, rows, cols), BF16),
            pltpu.VMEM((4, rows, cols), BF16),
            pltpu.VMEM((4, rows, cols), BF16),
            dma((8,)), dma((5,)), dma((4,)),
            dma((2, terms)), dma((3, terms)), dma((4, terms)),
            dma((slots, moved)), dma((slots, moved)),
            dma((4, 4)), dma((4, 4)), dma((4,)), dma((4,)), dma((2,)),
        ],
        compiler_params=pltpu.CompilerParams(
            has_side_effects=True, collective_id=0, vmem_limit_bytes=60 * 2**20
        ),
    )(dims, channel_term, channel_out, coefs, state, right, left)


def passed_along(value, axis, steps):
    count = lax.axis_size(axis)
    first, last = (max(0, -steps), min(count, count - steps))
    return lax.ppermute(value, axis, [(source, source + steps) for source in range(first, last)])


def gathered_apply(sector, live_dim, wave, right, combined, rows, slots):
    width = wave.shape[1]
    terms = right.shape[0]
    whole_state = lax.all_gather(wave, "pan", axis=0, tiled=True)
    indices = lax.iota(jnp.int32, width)
    inside = (indices[:, None] < live_dim) & (indices[None, :] < live_dim)
    masked = jnp.where(inside, whole_state, jnp.zeros((), BF16))
    right_full = lax.all_gather(right, "pan", axis=2, tiled=True)
    term_full = jnp.einsum("ik,wkq->wiq", masked, right_full, preferred_element_type=F32).astype(BF16)
    parts = jnp.einsum(
        "wjri,wiq->jrq", combined.reshape(terms, slots, rows, width), term_full,
        preferred_element_type=F32,
    )
    collected = parts[2]
    for offset in OFFSETS:
        collected = collected + passed_along(parts[offset + 2], "sec", offset)
    return collected


def on_device(
    wave_state, right_blocks, left_blocks, coupling, channel_term, channel_out, sector_dims
):
    rows, width = wave_state.shape[1:]
    terms = right_blocks.shape[1]
    slots = 5
    sector = lax.axis_index("sec")
    live_dim = sector_dims[0]
    if lax.axis_size("pan") == 4 and right_blocks.shape[3] % 128 == 0:
        collected = line_apply(
            lax.axis_size("sec"), slots, sector_dims, channel_term, channel_out, coupling,
            wave_state[0], right_blocks[0], left_blocks,
        )
    else:
        cells = channel_term * slots + channel_out - sector + 2
        coefs = coupling.astype(F32)
        combined = combine(cells, coefs, left_blocks, terms * slots)
        collected = gathered_apply(
            sector, live_dim, wave_state[0], right_blocks[0], combined, rows, slots
        )
    indices = lax.iota(jnp.int32, width)
    row_ids = lax.axis_index("pan") * rows + lax.iota(jnp.int32, rows)
    kept_mask = (row_ids[:, None] < live_dim) & (indices[None, :] < live_dim)
    return jnp.where(kept_mask, collected, jnp.zeros((), F32))[None]


def solution(mesh):
    return jax.shard_map(
        on_device,
        mesh=mesh,
        in_specs=(
            P("sec", "pan", None),
            P("sec", None, None, "pan"),
            P("sec", "pan", None),
            P("sec"),
            P("sec"),
            P("sec"),
            P("sec"),
        ),
        out_specs=P("sec", "pan", None),
        check_vma=False,
    )
```

time: 147 us -> 126 us (0.86); the launches traced: 145 us -> 126 us
  Pallas kernels: 141 us -> 123 us
    pallas_call x1, Pallas kernels: 136 us -> 123 us  [line_apply(): pl.pallas_call(functools.partial(line_kernel, sectors, moved), out_shape=...]
    pallas_call x1 -> x0, Pallas kernels: 5.46 us -> none  [order_channels(): pl.pallas_call(functools.partial(order_kernel, slots), out_shape=(jax.Sha...]
where the time goes in v1:
time: 126 us
  Pallas kernels  123 us (98%)
  other arithmetic  1.76 us (1%)
    pallas_call x1, Pallas kernels, line_apply(): pl.pallas_call(functools.partial(line_kernel, sectors, moved), out_shape=...  123 us

profile of v1, /device:TPU:0, one launch (start us, length us, event | category | flops | bytes accessed | tf_op | source)
XLA Modules:
  0.0 125.9 jit_solution(5557422046966855500)
XLA Ops:
  0.7 123.4 %shard_map.73 = f32[128,512]{1,0:T(8,128)} custom-call(s32[1]{0:T(128)} %copy.8.dims_ref, s32[72]{0:T(128)} %term_ref.1, s32[72]{0:T(128)} %out_id_ref.1, bf16[72]{0:T(256)(128)(2,1)} %coef_ref.1, bf16[128,512]{1,0:T(8,128)(2,1)} %bitcast.8, bf16[16,512,128]{2,1,0:T(8,128)(2,1)} %bitcast.7, bf16[72,128,512]{2,1,0:T(8,128)(2,1)} %left_ref.1), custom_call_target="tpu_custom_call" | custom-call | tf_op jit(solution)/shard_map/pallas_call | solution.py:488
  124.1 1.7 %select_bitcast_fusion = f32[1,128,512]{2,1,0:T(8,128)} fusion(f32[128,512]{1,0:T(8,128)} %shard_map.73, pred[512]{0:T(512)(128)(4,1)S(1)} %iota_compare_fusion, pred[128]{0:T(512)(128)(4,1)S(1)} %add_compare_fusion), kind=kLoop, calls=%fused_computation | loop fusion | flops 131072 | bytes 524928 | tf_op jit(solution)/shard_map/broadcast_in_dim | solution.py:579
  (2 shorter events, 0.0 us)

commit v2 on v1

--- a/solution.py
+++ b/solution.py
@@ -487,7 +487,7 @@
     any_space = pl.BlockSpec(memory_space=pl.ANY)
     return pl.pallas_call(
         functools.partial(line_kernel, sectors, moved),
-        out_shape=jax.ShapeDtypeStruct((rows, width), F32),
+        out_shape=pltpu.VMEM((rows, width), F32),
         in_specs=[any_space] * 7,
         out_specs=pl.BlockSpec(memory_space=pltpu.VMEM),
         scratch_shapes=[

time: 126 us -> 124 us (0.984)
  no operation moved by 1% of the time
where the time goes in v2:
time: 124 us
  Pallas kernels  123 us (99%)
    pallas_call x1, Pallas kernels, line_apply(): pl.pallas_call(functools.partial(line_kernel, sectors, moved), out_shape=...  123 us

profile of v2, /device:TPU:0, one launch (start us, length us, event | category | flops | bytes accessed | tf_op | source)
XLA Modules:
  0.0 124.3 jit_solution(1078663545318055467)
XLA Ops:
  0.7 122.8 %shard_map.73 = f32[128,512]{1,0:T(8,128)S(1)} custom-call(s32[1]{0:T(128)} %copy.8.dims_ref, s32[72]{0:T(128)} %term_ref.1, s32[72]{0:T(128)} %out_id_ref.1, bf16[72]{0:T(256)(128)(2,1)} %coef_ref.1, bf16[128,512]{1,0:T(8,128)(2,1)} %bitcast.8, bf16[16,512,128]{2,1,0:T(8,128)(2,1)} %bitcast.7, bf16[72,128,512]{2,1,0:T(8,128)(2,1)} %left_ref.1), custom_call_target="tpu_custom_call" | custom-call | tf_op jit(solution)/shard_map/pallas_call | solution.py:488
  123.5 0.8 select_bitcast_fusion
  (2 shorter events, 0.0 us)

commit v3 on v2

--- a/solution.py
+++ b/solution.py
@@ -80,11 +80,11 @@
 
 
 def line_kernel(
-    sectors, moved, dims_ref, term_ref, out_id_ref, coef_ref, state_ref, right_ref, left_ref,
+    sectors, dims_ref, term_ref, out_id_ref, coef_ref, state_ref, right_ref, left_ref,
     out_ref,
     dims, term_ids, out_ids, coef, table, spots, coefs, kept, filled,
     left_all, running, summed,
-    state_all, masked, gathered, comb, comb_end, kept_terms, acc, acc_end,
+    state_all, masked, gathered, blocks, comb, comb_end, acc, acc_end,
     stage, landed, stage_end, landed_end, back, back_landed,
     local_sems, state_send, state_recv, own_send, relay_send, right_recv,
     end_send, end_recv, part_send, part_recv, part_end_send, part_end_recv, back_sems,
@@ -101,6 +101,12 @@
     other_mid = jnp.where(me <= 1, 2, 1)
     far_end = 3 - near_end
     near_mid = jnp.where(me <= 1, 1, 2)
+    per = comb_end.shape[2]
+    groups = terms // per
+    early = 1
+    inner = width - rows
+    near_rows = pl.ds(pl.multiple_of(jnp.where(near_end == 0, 0, rows), rows), inner)
+    far_rows = pl.ds(pl.multiple_of(far_end * rows, rows), rows)
 
     def remote(src, dst, send, recv, where, axis="pan"):
         return pltpu.make_async_remote_copy(
@@ -128,11 +134,18 @@
         block = gathered.at[owner, term]
         return remote(block, block, relay_send.at[way, term], right_recv.at[owner, term], where)
 
-    def end_copy(slot, term, where):
+    def block_copy(sems, way, owner, term, where):
+        block = blocks.at[owner, term, near_rows]
+        return remote(block, block, sems.at[way, term], right_recv.at[owner, term], where)
+
+    def block_arrived(owner, term):
+        block_copy(relay_send, 0, owner, term, me).wait_recv()
+
+    def end_copy(slot, group, where):
         spot = pl.ds(pl.multiple_of(slot * rows, rows), rows)
         return remote(
-            comb.at[term, spot], comb_end.at[slot, term],
-            end_send.at[slot, term], end_recv.at[slot, term], where,
+            comb.at[pl.ds(group * per, per), spot, far_rows], comb_end.at[slot, group],
+            end_send.at[slot, group], end_recv.at[slot, group], where,
         )
 
     def arrived(owner, term):
@@ -145,10 +158,11 @@
             part_send.at[index, owner], part_recv.at[index, owner], sector + OFFSETS[index], "sec",
         )
 
-    def part_end_copy(index):
+    def part_end_copy(index, owner):
         return remote(
-            stage_end.at[index], landed_end.at[index],
-            part_end_send.at[index], part_end_recv.at[index], sector + OFFSETS[index], "sec",
+            stage_end.at[index, owner], landed_end.at[index, owner],
+            part_end_send.at[index, owner], part_end_recv.at[index, owner],
+            sector + OFFSETS[index], "sec",
         )
 
     def back_copy(where):
@@ -185,8 +199,6 @@
 
     pl.semaphore_wait(barrier, peers)
 
-    early = min(2, terms - moved)
-
     @pl.when(is_mid)
     def _():
         state_own(0, near_end).start()
@@ -194,7 +206,10 @@
 
         @pl.loop(0, early)
         def _(term):
-            own_copy(1, moved + term, near_end).start()
+            own_copy(1, term, near_end).start()
+
+        @pl.loop(0, 2 * early)
+        def _(term):
             own_copy(0, term, other_mid).start()
 
     @pl.when(is_end)
@@ -227,7 +242,23 @@
     acc_end[...] = jnp.zeros_like(acc_end)
     running[...] = jnp.zeros_like(running)
 
-    later = min(early + 3, terms - moved)
+    live = dims[0]
+    inside_col = lax.broadcasted_iota(jnp.int32, (rows, width), 1) < live
+
+    def mask_rows(owner):
+        row = lax.broadcasted_iota(jnp.int32, (rows, width), 0) + owner * rows
+        spot = pl.ds(pl.multiple_of(owner * rows, rows), rows)
+        masked[spot, :] = jnp.where(
+            inside_col & (row < live), state_all[owner].astype(F32), 0.0
+        ).astype(BF16)
+
+    def block_of(owner, term, spot):
+        return jnp.dot(
+            masked[spot, :], gathered[owner, term], preferred_element_type=F32
+        ).astype(BF16)
+
+    large[1].wait()
+    large[2].wait()
 
     @pl.when(is_mid)
     def _():
@@ -236,18 +267,21 @@
         state_wait(near_end)
         state_relay(3, near_end, other_mid).start()
 
-        @pl.loop(early, later)
-        def _(term):
-            own_copy(1, moved + term, near_end).start()
+        @pl.loop(2 * early, terms)
+        def _(term):
+            own_copy(0, term, other_mid).start()
+
+        @pl.loop(0, 3)
+        def _(which):
+            mask_rows(jnp.where(which == 0, me, jnp.where(which == 1, other_mid, near_end)))
 
         @pl.loop(early, terms)
         def _(term):
-            own_copy(0, term, other_mid).start()
+            blocks[me, term, near_rows, :] = block_of(me, term, near_rows)
+            block_copy(own_send, 1, me, term, near_end).start()
 
     spots_copy.wait()
-    for copy in large:
-        copy.wait()
-
+    large[0].wait()
     channels = left_all.shape[0]
 
     def inside(spot):
@@ -267,38 +301,12 @@
             value = summed[inside(spots[1, cell])].astype(F32) * filled[pl.ds(cell, 1), :]
             comb[term, slot * rows:(slot + 1) * rows, :] = value.astype(BF16)
 
-    @pl.when(is_mid)
-    def _():
-        state_wait(far_end)
-        state_relay(4, far_end, near_end).start()
-
-        @pl.loop(later, terms - moved)
-        def _(term):
-            own_copy(1, moved + term, near_end).start()
-
     @pl.when(is_end)
     def _():
         for slot in END_SLOTS:
-            @pl.loop(0, moved)
-            def _(term):
-                end_copy(slot, term, near_mid).start()
-
-        for owner in (near_mid, 3 - near_mid, 3 - me):
-            state_wait(owner)
-
-    live = dims[0]
-    inside_col = lax.broadcasted_iota(jnp.int32, (rows, width), 1) < live
-    for owner in range(4):
-        row = lax.broadcasted_iota(jnp.int32, (rows, width), 0) + owner * rows
-        masked[owner * rows:(owner + 1) * rows, :] = jnp.where(
-            inside_col & (row < live), state_all[owner].astype(F32), 0.0
-        ).astype(BF16)
-
-    def multiply(owner, term, keep=False):
-        block = jnp.dot(masked[...], gathered[owner, term], preferred_element_type=F32).astype(BF16)
-        if keep:
-            kept_terms[term, owner] = block
-        acc[owner] += jnp.dot(comb[term], block, preferred_element_type=F32)
+            @pl.loop(0, groups)
+            def _(group):
+                end_copy(slot, group, near_mid).start()
 
     def send_parts(owner):
         for index in range(4):
@@ -322,71 +330,106 @@
             def _():
                 out_ref[:, spot * cols:(spot + 1) * cols] = acc[spot, home * rows:(home + 1) * rows, :]
 
-    def end_slot(slot):
-        @pl.loop(0, moved)
-        def _(term):
-            end_copy(slot, term, me).wait_recv()
+    def end_multiply(slot, group, owner):
+        left = [comb_end[slot, group, spot] for spot in range(per)]
+        right = [blocks[owner, group * per + spot, far_rows, :] for spot in range(per)]
+        acc_end[slot, owner] += jnp.dot(
+            jnp.concatenate(left, axis=1), jnp.concatenate(right, axis=0),
+            preferred_element_type=F32,
+        )
+
+    def send_end_parts(index, owner):
+        @pl.when(goes(index))
+        def _():
+            stage_end[index, owner] = acc_end[OFFSETS[index] + 2, owner].astype(BF16)
+            part_end_copy(index, owner).start()
+
+    @pl.when(is_mid)
+    def _():
+        def near_owner(which):
+            return jnp.where(which == 0, me, jnp.where(which == 1, other_mid, near_end))
+
+        def multiply(owner, term):
+            acc[owner] += jnp.dot(comb[term], blocks[owner, term], preferred_element_type=F32)
+
+        state_wait(far_end)
+        mask_rows(far_end)
+
+        @pl.loop(0, early)
+        def _(term):
+            blocks[me, term, near_rows, :] = block_of(me, term, near_rows)
+
+        @pl.loop(0, terms)
+        def _(term):
+            blocks[me, term, far_rows, :] = block_of(me, term, far_rows)
+
+        everything = slice(None)
+
+        @pl.loop(0, terms)
+        def _(term):
+            arrived(other_mid, term)
+            blocks[other_mid, term] = block_of(other_mid, term, everything)
+            block_copy(relay_send, 0, other_mid, term, near_end).start()
+            arrived(near_end, term)
+            relay_copy(1, near_end, term, other_mid).start()
+            blocks[near_end, term] = block_of(near_end, term, everything)
+
+            @pl.loop(0, 3)
+            def _(which):
+                multiply(near_owner(which), term)
+
+        @pl.loop(0, 3)
+        def _(which):
+            send_parts(near_owner(which))
+
+        @pl.loop(0, terms)
+        def _(term):
+            arrived(far_end, term)
+            blocks[far_end, term] = block_of(far_end, term, everything)
+            block_copy(relay_send, 2, far_end, term, near_end).start()
+            multiply(far_end, term)
+
+            for index in range(4):
+                slot = OFFSETS[index] + 2
+
+                @pl.when(term == (index + 1) * terms // 4 - 1)
+                def _():
+                    @pl.loop(0, groups)
+                    def _(group):
+                        end_copy(slot, group, me).wait_recv()
+
+                        @pl.loop(0, 3)
+                        def _(which):
+                            end_multiply(slot, group, near_owner(which))
+
+                    @pl.loop(0, 3)
+                    def _(which):
+                        send_end_parts(index, near_owner(which))
+
+        send_parts(far_end)
+
+        for index in range(4):
+            @pl.loop(0, groups)
+            def _(group):
+                end_multiply(OFFSETS[index] + 2, group, far_end)
+
+            send_end_parts(index, far_end)
+
+        @pl.loop(0, groups)
+        def _(group):
+            end_copy(home, group, me).wait_recv()
 
             @pl.loop(0, 4)
             def _(owner):
-                acc_end[slot, owner] += jnp.dot(
-                    comb_end[slot, term], kept_terms[term, owner], preferred_element_type=F32
-                )
-
-    @pl.when(is_mid)
-    def _():
-        def first_pass(begin, end, keep):
-            @pl.loop(begin, end)
-            def _(term):
-                arrived(other_mid, term)
-                if not keep:
-                    relay_copy(0, other_mid, term, near_end).start()
-                arrived(near_end, term)
-                relay_copy(1, near_end, term, other_mid).start()
-
-                @pl.loop(0, 3)
-                def _(which):
-                    owner = jnp.where(which == 0, me, jnp.where(which == 1, other_mid, near_end))
-                    multiply(owner, term, keep)
-
-        first_pass(0, moved, True)
-        first_pass(moved, terms, False)
-
-        @pl.loop(0, 3)
-        def _(which):
-            send_parts(jnp.where(which == 0, me, jnp.where(which == 1, other_mid, near_end)))
-
-        @pl.loop(0, moved)
-        def _(term):
-            arrived(far_end, term)
-            multiply(far_end, term, True)
-
-        @pl.loop(moved, terms)
-        def _(term):
-            arrived(far_end, term)
-            relay_copy(2, far_end, term, near_end).start()
-            multiply(far_end, term)
-
-            for index in range(4):
-                slot = OFFSETS[index] + 2
-
-                @pl.when(term == turn_of(index, moved, terms))
-                def _():
-                    end_slot(slot)
-
-                    @pl.when(goes(index))
-                    def _():
-                        stage_end[index] = acc_end[slot].astype(BF16)
-                        part_end_copy(index).start()
-
-        send_parts(far_end)
-        end_slot(home)
+                end_multiply(home, group, owner)
 
         for index in range(4):
             @pl.when(comes(index))
             def _():
-                part_end_copy(index).wait_recv()
-                acc_end[home] += landed_end[index].astype(F32)
+                @pl.loop(0, 4)
+                def _(owner):
+                    part_end_copy(index, owner).wait_recv()
+                    acc_end[home, owner] += landed_end[index, owner].astype(F32)
 
         back[...] = acc_end[home].astype(BF16)
         back_copy(near_end).start()
@@ -399,18 +442,35 @@
     @pl.when(is_end)
     def _():
         turn = jnp.where(me == 0, 1, -1)
-
-        @pl.loop(0, 4)
+        state_wait(near_mid)
+        state_wait(3 - near_mid)
+
+        @pl.loop(0, 3)
+        def _(rank):
+            mask_rows(me + turn * rank)
+
+        def multiply(owner, term, block):
+            acc[owner] += jnp.dot(comb[term, :, near_rows], block, preferred_element_type=F32)
+
+        @pl.loop(0, terms)
+        def _(term):
+            multiply(me, term, block_of(me, term, near_rows))
+
+        send_parts(me)
+
+        @pl.loop(0, early)
+        def _(term):
+            arrived(near_mid, term)
+            multiply(near_mid, term, block_of(near_mid, term, near_rows))
+
+        @pl.loop(1, 4)
         def _(rank):
             owner = me + turn * rank
 
-            @pl.loop(moved, terms)
+            @pl.loop(jnp.where(rank == 1, early, 0), terms)
             def _(term):
-                @pl.when(rank > 0)
-                def _():
-                    arrived(owner, term)
-
-                multiply(owner, term)
+                block_arrived(owner, term)
+                multiply(owner, term, blocks[owner, term, near_rows, :])
 
             send_parts(owner)
 
@@ -432,9 +492,9 @@
             def _(owner):
                 part_copy(index, owner).wait_send()
 
-            @pl.when(is_mid)
-            def _():
-                part_end_copy(index).wait_send()
+                @pl.when(is_mid)
+                def _():
+                    part_end_copy(index, owner).wait_send()
 
     @pl.when(is_mid)
     def _():
@@ -442,18 +502,21 @@
         state_own(1, other_mid).wait_send()
         state_relay(2, other_mid, near_end).wait_send()
         state_relay(3, near_end, other_mid).wait_send()
-        state_relay(4, far_end, near_end).wait_send()
+
+        @pl.loop(0, early)
+        def _(term):
+            own_copy(1, term, near_end).wait_send()
+
+        @pl.loop(early, terms)
+        def _(term):
+            block_copy(own_send, 1, me, term, near_end).wait_send()
 
         @pl.loop(0, terms)
         def _(term):
             own_copy(0, term, other_mid).wait_send()
             relay_copy(1, near_end, term, other_mid).wait_send()
-
-            @pl.when(term >= moved)
-            def _():
-                own_copy(1, term, near_end).wait_send()
-                relay_copy(0, other_mid, term, near_end).wait_send()
-                relay_copy(2, far_end, term, near_end).wait_send()
+            block_copy(relay_send, 0, other_mid, term, near_end).wait_send()
+            block_copy(relay_send, 2, far_end, term, near_end).wait_send()
 
         back_copy(near_end).wait_send()
 
@@ -466,14 +529,9 @@
             own_copy(0, term, near_mid).wait_send()
 
         for slot in END_SLOTS:
-            @pl.loop(0, moved)
-            def _(term):
-                end_copy(slot, term, near_mid).wait_send()
-
-
-def turn_of(index, moved, terms):
-    steps = terms - moved
-    return moved + min(steps - 1, max(0, (steps * (4 * index - 2)) // 12))
+            @pl.loop(0, groups)
+            def _(group):
+                end_copy(slot, group, near_mid).wait_send()
 
 
 def line_apply(sectors, slots, dims, channel_term, channel_out, coefs, state, right, left):
@@ -481,12 +539,13 @@
     rows = state.shape[0]
     channels = left.shape[0]
     cells = slots * terms
-    moved = max(1, terms // 4)
+    per = 4
+    groups = terms // per
     tall = slots * rows
     dma = pltpu.SemaphoreType.DMA
     any_space = pl.BlockSpec(memory_space=pl.ANY)
     return pl.pallas_call(
-        functools.partial(line_kernel, sectors, moved),
+        functools.partial(line_kernel, sectors),
         out_shape=pltpu.VMEM((rows, width), F32),
         in_specs=[any_space] * 7,
         out_specs=pl.BlockSpec(memory_space=pltpu.VMEM),
@@ -506,9 +565,9 @@
             pltpu.VMEM((4, rows, width), BF16),
             pltpu.VMEM((width, width), BF16),
             pltpu.VMEM((4, terms, width, cols), BF16),
+            pltpu.VMEM((4, terms, width, cols), BF16),
             pltpu.VMEM((terms, tall, width), BF16),
-            pltpu.VMEM((slots, moved, rows, width), BF16),
-            pltpu.VMEM((moved, 4, width, cols), BF16),
+            pltpu.VMEM((slots, groups, per, rows, rows), BF16),
             pltpu.VMEM((4, tall, cols), F32),
             pltpu.VMEM((slots, 4, rows, cols), F32),
             pltpu.VMEM((4, 4, rows, cols), BF16),
@@ -517,10 +576,10 @@
             pltpu.VMEM((4, 4, rows, cols), BF16),
             pltpu.VMEM((4, rows, cols), BF16),
             pltpu.VMEM((4, rows, cols), BF16),
-            dma((8,)), dma((5,)), dma((4,)),
+            dma((8,)), dma((4,)), dma((4,)),
             dma((2, terms)), dma((3, terms)), dma((4, terms)),
-            dma((slots, moved)), dma((slots, moved)),
-            dma((4, 4)), dma((4, 4)), dma((4,)), dma((4,)), dma((2,)),
+            dma((slots, groups)), dma((slots, groups)),
+            dma((4, 4)), dma((4, 4)), dma((4, 4)), dma((4, 4)), dma((2,)),
         ],
         compiler_params=pltpu.CompilerParams(
             has_side_effects=True, collective_id=0, vmem_limit_bytes=60 * 2**20
@@ -561,7 +620,7 @@
     slots = 5
     sector = lax.axis_index("sec")
     live_dim = sector_dims[0]
-    if lax.axis_size("pan") == 4 and right_blocks.shape[3] % 128 == 0:
+    if lax.axis_size("pan") == 4 and right_blocks.shape[3] % 128 == 0 and terms % 4 == 0:
         collected = line_apply(
             lax.axis_size("sec"), slots, sector_dims, channel_term, channel_out, coupling,
             wave_state[0], right_blocks[0], left_blocks,

time: 124 us -> 122 us (0.984)
  Pallas kernels: 123 us -> 120 us
    pallas_call x1, Pallas kernels: 123 us -> 120 us  [line_apply(): pl.pallas_call(functools.partial(line_kernel, sectors), out_shape=pltpu.V...]
where the time goes in v3:
time: 122 us
  Pallas kernels  120 us (98%)
    pallas_call x1, Pallas kernels, line_apply(): pl.pallas_call(functools.partial(line_kernel, sectors), out_shape=pltpu.V...  120 us

profile of v3, /device:TPU:0, one launch (start us, length us, event | category | flops | bytes accessed | tf_op | source)
XLA Modules:
  0.0 121.6 jit_solution(15018264068370704424)
XLA Ops:
  0.7 120.1 %shard_map.73 = f32[128,512]{1,0:T(8,128)S(1)} custom-call(s32[1]{0:T(128)} %copy.8.dims_ref, s32[72]{0:T(128)} %term_ref.1, s32[72]{0:T(128)} %out_id_ref.1, bf16[72]{0:T(256)(128)(2,1)} %coef_ref.1, bf16[128,512]{1,0:T(8,128)(2,1)} %bitcast.8, bf16[16,512,128]{2,1,0:T(8,128)(2,1)} %bitcast.7, bf16[72,128,512]{2,1,0:T(8,128)(2,1)} %left_ref.1), custom_call_target="tpu_custom_call" | custom-call | tf_op jit(solution)/shard_map/pallas_call | solution.py:547
  120.8 0.8 select_bitcast_fusion
  (2 shorter events, 0.0 us)

commit v4 on v3

--- a/solution.py
+++ b/solution.py
@@ -8,7 +8,7 @@
 from jax.sharding import PartitionSpec as P
 
 OFFSETS = (-2, -1, 1, 2)
-END_SLOTS = (0, 1, 3, 4, 2)
+END_SLOTS = (0, 1, 3, 4)
 F32 = jnp.float32
 BF16 = jnp.bfloat16
 
@@ -80,14 +80,15 @@
 
 
 def line_kernel(
-    sectors, dims_ref, term_ref, out_id_ref, coef_ref, state_ref, right_ref, left_ref,
+    sectors, detours, least, dims_ref, term_ref, out_id_ref, coef_ref, state_ref, right_ref, left_ref,
     out_ref,
     dims, term_ids, out_ids, coef, table, spots, coefs, kept, filled,
     left_all, running, summed,
-    state_all, masked, gathered, blocks, comb, comb_end, acc, acc_end,
+    state_all, masked, gathered, blocks, comb, comb_end, comb_extra, passing, acc, acc_end,
     stage, landed, stage_end, landed_end, back, back_landed,
     local_sems, state_send, state_recv, own_send, relay_send, right_recv,
-    end_send, end_recv, part_send, part_recv, part_end_send, part_end_recv, back_sems,
+    end_send, end_recv, extra_send, extra_recv, home_send, home_recv,
+    passing_send, passing_recv, part_send, part_recv, part_end_send, part_end_recv, back_sems,
 ):
     terms, width, cols = right_ref.shape
     rows = state_ref.shape[0]
@@ -103,10 +104,20 @@
     near_mid = jnp.where(me <= 1, 1, 2)
     per = comb_end.shape[2]
     groups = terms // per
-    early = 1
+    edge = (sector < 2) | (sector >= sectors - 2)
+    cut = terms - jnp.where(edge, comb_extra.shape[1], least)
+    turned = terms - detours
+    low = sector < sectors // 2
+    outer = jnp.where(low, sector - 2, sector + 2)
+    served = jnp.where(low, sector + 2, sector - 2)
+    strips = home_send.shape[0]
+    strip = rows // strips
+    half = rows // 2
     inner = width - rows
     near_rows = pl.ds(pl.multiple_of(jnp.where(near_end == 0, 0, rows), rows), inner)
     far_rows = pl.ds(pl.multiple_of(far_end * rows, rows), rows)
+    short_rows = pl.ds(pl.multiple_of(jnp.where(near_end == 0, 0, 2 * rows), rows), inner - rows)
+    extra_rows = pl.ds(pl.multiple_of(other_mid * rows, rows), rows)
 
     def remote(src, dst, send, recv, where, axis="pan"):
         return pltpu.make_async_remote_copy(
@@ -114,32 +125,65 @@
             device_id={axis: where}, device_id_type=pl.DeviceIdType.MESH,
         )
 
-    def state_own(way, where):
-        return remote(state_ref, state_all.at[me], state_send.at[way], state_recv.at[me], where)
-
-    def state_relay(way, owner, where):
-        block = state_all.at[owner]
-        return remote(block, block, state_send.at[way], state_recv.at[owner], where)
+    def state_copy(way, owner, part, where):
+        block = state_all.at[owner, pl.ds(part * half, half)]
+        return remote(
+            block, block, state_send.at[way, part], state_recv.at[owner, part], where
+        )
 
     def state_wait(owner):
-        state_relay(0, owner, me).wait_recv()
-
-    def own_copy(way, term, where):
+        for part in range(2):
+            state_copy(0, owner, part, me).wait_recv()
+
+    def own_copy(term, where):
         return remote(
             right_ref.at[term], gathered.at[me, term],
-            own_send.at[way, term], right_recv.at[me, term], where,
-        )
-
-    def relay_copy(way, owner, term, where):
+            own_send.at[0, term], right_recv.at[me, term], where,
+        )
+
+    def relay_copy(owner, term, where):
         block = gathered.at[owner, term]
-        return remote(block, block, relay_send.at[way, term], right_recv.at[owner, term], where)
-
-    def block_copy(sems, way, owner, term, where):
-        block = blocks.at[owner, term, near_rows]
+        return remote(block, block, relay_send.at[1, term], right_recv.at[owner, term], where)
+
+    def block_copy(sems, way, owner, term, where, spot):
+        block = blocks.at[owner, term, spot]
         return remote(block, block, sems.at[way, term], right_recv.at[owner, term], where)
 
-    def block_arrived(owner, term):
-        block_copy(relay_send, 0, owner, term, me).wait_recv()
+    def send_block(sems, way, owner, term):
+        @pl.when(term < cut)
+        def _():
+            block_copy(sems, way, owner, term, near_end, near_rows).start()
+
+        @pl.when(term >= cut)
+        def _():
+            block_copy(sems, way, owner, term, near_end, short_rows).start()
+
+    def sent_block(sems, way, owner, term):
+        @pl.when(term < cut)
+        def _():
+            block_copy(sems, way, owner, term, near_end, near_rows).wait_send()
+
+        @pl.when(term >= cut)
+        def _():
+            block_copy(sems, way, owner, term, near_end, short_rows).wait_send()
+
+    def turn_off(term):
+        index = term - turned
+        return remote(
+            blocks.at[me, term, near_rows], passing.at[index],
+            passing_send.at[0, index], passing_recv.at[index], outer, "sec",
+        )
+
+    def pass_on(term):
+        index = term - turned
+        return pltpu.make_async_remote_copy(
+            src_ref=passing.at[index], dst_ref=blocks.at[me, term, near_rows],
+            send_sem=passing_send.at[1, index], recv_sem=right_recv.at[me, term],
+            device_id={"sec": served, "pan": near_end}, device_id_type=pl.DeviceIdType.MESH,
+        )
+
+    def block_arrived(owner, term, spot):
+        block_copy(relay_send, 0, owner, term, me, spot).wait_recv()
 
     def end_copy(slot, group, where):
         spot = pl.ds(pl.multiple_of(slot * rows, rows), rows)
@@ -148,6 +192,22 @@
             end_send.at[slot, group], end_recv.at[slot, group], where,
         )
 
+    def extra_copy(slot, term, where):
+        spot = pl.ds(pl.multiple_of(slot * rows, rows), rows)
+        index = terms - 1 - term
+        return remote(
+            comb.at[term, spot, extra_rows], comb_extra.at[slot, index],
+            extra_send.at[slot, index], extra_recv.at[slot, index], where,
+        )
+
+    def home_copy(part, group, where):
+        source = pl.ds(home * rows + part * strip, strip)
+        spot = pl.ds(part * strip, strip)
+        return remote(
+            comb.at[pl.ds(group * per, per), source, far_rows], comb_end.at[home, group, :, spot],
+            home_send.at[part, group], home_recv.at[part, group], where,
+        )
+
     def arrived(owner, term):
         block = gathered.at[owner, term]
         remote(block, block, relay_send.at[0, term], right_recv.at[owner, term], me).wait_recv()
@@ -165,8 +225,12 @@
             sector + OFFSETS[index], "sec",
         )
 
-    def back_copy(where):
-        return remote(back, back_landed, back_sems.at[0], back_sems.at[1], where)
+    def back_copy(part, where):
+        spot = pl.ds(part * strip, strip)
+        return remote(
+            back.at[:, spot], back_landed.at[:, spot],
+            back_sems.at[0, part], back_sems.at[1, part], where,
+        )
 
     def goes(index):
         target = sector + OFFSETS[index]
@@ -175,50 +239,6 @@
     def comes(index):
         source = sector - OFFSETS[index]
         return (source >= 0) & (source < sectors)
-
-    barrier = pltpu.get_barrier_semaphore()
-
-    def greet(axis, where):
-        pl.semaphore_signal(
-            barrier, inc=1, device_id={axis: where}, device_id_type=pl.DeviceIdType.MESH
-        )
-
-    greet("pan", jnp.where(is_mid, near_end, near_mid))
-
-    @pl.when(is_mid)
-    def _():
-        greet("pan", other_mid)
-
-    peers = jnp.where(is_mid, 2, 1)
-    for index in range(4):
-        peers = peers + goes(index).astype(jnp.int32)
-
-        @pl.when(goes(index))
-        def _():
-            greet("sec", sector + OFFSETS[index])
-
-    pl.semaphore_wait(barrier, peers)
-
-    @pl.when(is_mid)
-    def _():
-        state_own(0, near_end).start()
-        state_own(1, other_mid).start()
-
-        @pl.loop(0, early)
-        def _(term):
-            own_copy(1, term, near_end).start()
-
-        @pl.loop(0, 2 * early)
-        def _(term):
-            own_copy(0, term, other_mid).start()
-
-    @pl.when(is_end)
-    def _():
-        state_own(0, near_mid).start()
-
-        @pl.loop(0, terms)
-        def _(term):
-            own_copy(0, term, near_mid).start()
 
     small = [
         pltpu.make_async_copy(dims_ref, dims, local_sems.at[0]),
@@ -231,8 +251,53 @@
         pltpu.make_async_copy(state_ref, state_all.at[me], local_sems.at[5]),
         pltpu.make_async_copy(right_ref, gathered.at[me], local_sems.at[6]),
     ]
-    for copy in small + large:
+    for copy in large[1:2] + small + large[2:] + large[:1]:
         copy.start()
+
+    barrier = pltpu.get_barrier_semaphore()
+
+    def greet(axis, where):
+        pl.semaphore_signal(
+            barrier, inc=1, device_id={axis: where}, device_id_type=pl.DeviceIdType.MESH
+        )
+
+    greet("pan", jnp.where(is_mid, near_end, near_mid))
+
+    @pl.when(is_mid)
+    def _():
+        greet("pan", other_mid)
+
+    peers = jnp.where(is_mid, 2, 1)
+    for index in range(4):
+        peers = peers + goes(index).astype(jnp.int32)
+
+        @pl.when(goes(index))
+        def _():
+            greet("sec", sector + OFFSETS[index])
+
+    pl.semaphore_wait(barrier, peers)
+
+    large[1].wait()
+
+    @pl.when(is_mid)
+    def _():
+        for part in range(2):
+            state_copy(0, me, part, near_end).start()
+            state_copy(1, me, part, other_mid).start()
+
+        @pl.loop(0, 2)
+        def _(term):
+            own_copy(term, other_mid).start()
+
+    @pl.when(is_end)
+    def _():
+        for part in range(2):
+            state_copy(0, me, part, near_mid).start()
+
+        @pl.loop(0, terms)
+        def _(term):
+            own_copy(term, near_mid).start()
+
     for copy in small:
         copy.wait()
     read_channels(slots, terms, sector, term_ids, out_ids, coef, coefs, kept, filled, table)
@@ -257,28 +322,36 @@
             masked[spot, :], gathered[owner, term], preferred_element_type=F32
         ).astype(BF16)
 
-    large[1].wait()
     large[2].wait()
 
     @pl.when(is_mid)
     def _():
-        state_wait(other_mid)
-        state_relay(2, other_mid, near_end).start()
-        state_wait(near_end)
-        state_relay(3, near_end, other_mid).start()
-
-        @pl.loop(2 * early, terms)
-        def _(term):
-            own_copy(0, term, other_mid).start()
+        for part in range(2):
+            state_copy(0, other_mid, part, me).wait_recv()
+            state_copy(2, other_mid, part, near_end).start()
+            state_copy(0, near_end, part, me).wait_recv()
+            state_copy(3, near_end, part, other_mid).start()
+
+        @pl.loop(2, terms)
+        def _(term):
+            own_copy(term, other_mid).start()
 
         @pl.loop(0, 3)
         def _(which):
             mask_rows(jnp.where(which == 0, me, jnp.where(which == 1, other_mid, near_end)))
 
-        @pl.loop(early, terms)
+        @pl.loop(0, terms)
         def _(term):
             blocks[me, term, near_rows, :] = block_of(me, term, near_rows)
-            block_copy(own_send, 1, me, term, near_end).start()
+            turns = jnp.logical_not(edge) & (term >= turned)
+
+            @pl.when(turns)
+            def _():
+                turn_off(term).start()
+
+            @pl.when(jnp.logical_not(turns))
+            def _():
+                send_block(own_send, 1, me, term)
 
     spots_copy.wait()
     large[0].wait()
@@ -303,19 +376,39 @@
 
     @pl.when(is_end)
     def _():
-        for slot in END_SLOTS:
+        for index, slot in enumerate(END_SLOTS):
+            @pl.when(goes(index))
+            def _():
+                @pl.loop(cut, terms)
+                def _(term):
+                    extra_copy(slot, term, near_mid).start()
+
+                @pl.loop(0, groups)
+                def _(group):
+                    end_copy(slot, group, near_mid).start()
+
+        @pl.loop(cut, terms)
+        def _(term):
+            extra_copy(home, term, near_mid).start()
+
+        @pl.loop(0, strips)
+        def _(part):
             @pl.loop(0, groups)
             def _(group):
-                end_copy(slot, group, near_mid).start()
+                home_copy(part, group, near_mid).start()
+
+    def across(index):
+        return (sector // 2 + (sector + OFFSETS[index]) // 2) % 4 == 3
 
     def send_parts(owner):
-        for index in range(4):
-            slot = OFFSETS[index] + 2
-
-            @pl.when(goes(index))
-            def _():
-                stage[index, owner] = acc[owner, slot * rows:(slot + 1) * rows, :].astype(BF16)
-                part_copy(index, owner).start()
+        for index, slot in enumerate(END_SLOTS):
+            stage[index, owner] = acc[owner, slot * rows:(slot + 1) * rows, :].astype(BF16)
+
+        for first in (True, False):
+            for index in range(4):
+                @pl.when(goes(index) & (across(index) == first))
+                def _():
+                    part_copy(index, owner).start()
 
     def take_parts(owner):
         for index in range(4):
@@ -330,13 +423,39 @@
             def _():
                 out_ref[:, spot * cols:(spot + 1) * cols] = acc[spot, home * rows:(home + 1) * rows, :]
 
-    def end_multiply(slot, group, owner):
-        left = [comb_end[slot, group, spot] for spot in range(per)]
-        right = [blocks[owner, group * per + spot, far_rows, :] for spot in range(per)]
-        acc_end[slot, owner] += jnp.dot(
-            jnp.concatenate(left, axis=1), jnp.concatenate(right, axis=0),
-            preferred_element_type=F32,
-        )
+    def far_blocks(owner, group):
+        return jnp.concatenate(
+            [blocks[owner, group * per + index, far_rows, :] for index in range(per)], axis=0
+        )
+
+    def end_rows(slot, group, spot):
+        return jnp.concatenate(
+            [comb_end[slot, group, index, spot, :] for index in range(per)], axis=1
+        )
+
+    def add_end(slot, owners, spot, left, rights):
+        for first in range(0, len(owners), 2):
+            pair = owners[first:first + 2]
+            product = jnp.dot(
+                left, jnp.concatenate(rights[first:first + 2], axis=1), preferred_element_type=F32
+            )
+            for index, owner in enumerate(pair):
+                acc_end[slot, owner, spot, :] += product[:, index * cols:(index + 1) * cols]
+
+    def end_multiply(slot, group, owners, spot=slice(None)):
+        rights = [far_blocks(owner, group) for owner in owners]
+        add_end(slot, owners, spot, end_rows(slot, group, spot), rights)
+
+    def extra_multiply(slot, owners, term):
+        rights = [blocks[owner, term, extra_rows, :] for owner in owners]
+        add_end(slot, owners, slice(None), comb_extra[slot, terms - 1 - term], rights)
+
+    def add_far(left, right):
+        product = jnp.dot(
+            jnp.concatenate(left, axis=0), right, preferred_element_type=F32
+        )
+        for index, slot in enumerate(END_SLOTS):
+            acc_end[slot, far_end] += product[index * rows:(index + 1) * rows]
 
     def send_end_parts(index, owner):
         @pl.when(goes(index))
@@ -352,12 +471,23 @@
         def multiply(owner, term):
             acc[owner] += jnp.dot(comb[term], blocks[owner, term], preferred_element_type=F32)
 
+        near_three = [me, other_mid, near_end]
+
+        for index, slot in enumerate(END_SLOTS):
+            @pl.when(jnp.logical_not(goes(index)))
+            def _():
+                comb_end[slot] = jnp.zeros(comb_end.shape[1:], BF16)
+                comb_extra[slot] = jnp.zeros(comb_extra.shape[1:], BF16)
+
         state_wait(far_end)
         mask_rows(far_end)
 
-        @pl.loop(0, early)
-        def _(term):
-            blocks[me, term, near_rows, :] = block_of(me, term, near_rows)
+        @pl.when(edge)
+        def _():
+            @pl.loop(turned, terms)
+            def _(term):
+                turn_off(term).wait_recv()
+                pass_on(term).start()
 
         @pl.loop(0, terms)
         def _(term):
@@ -369,9 +499,9 @@
         def _(term):
             arrived(other_mid, term)
             blocks[other_mid, term] = block_of(other_mid, term, everything)
-            block_copy(relay_send, 0, other_mid, term, near_end).start()
+            send_block(relay_send, 0, other_mid, term)
             arrived(near_end, term)
-            relay_copy(1, near_end, term, other_mid).start()
+            relay_copy(near_end, term, other_mid).start()
             blocks[near_end, term] = block_of(near_end, term, everything)
 
             @pl.loop(0, 3)
@@ -386,42 +516,73 @@
         def _(term):
             arrived(far_end, term)
             blocks[far_end, term] = block_of(far_end, term, everything)
-            block_copy(relay_send, 2, far_end, term, near_end).start()
+            send_block(relay_send, 2, far_end, term)
             multiply(far_end, term)
 
             for index in range(4):
                 slot = OFFSETS[index] + 2
 
-                @pl.when(term == (index + 1) * terms // 4 - 1)
+                @pl.when((term == (index + 1) * terms // 4 - 2) & goes(index))
                 def _():
+                    @pl.loop(cut, terms)
+                    def _(late):
+                        extra_copy(slot, late, me).wait_recv()
+                        extra_multiply(slot, near_three, late)
+
                     @pl.loop(0, groups)
                     def _(group):
                         end_copy(slot, group, me).wait_recv()
 
-                        @pl.loop(0, 3)
-                        def _(which):
-                            end_multiply(slot, group, near_owner(which))
+                        end_multiply(slot, group, near_three)
 
                     @pl.loop(0, 3)
                     def _(which):
                         send_end_parts(index, near_owner(which))
 
+        @pl.loop(cut, terms)
+        def _(term):
+            add_far(
+                [comb_extra[slot, terms - 1 - term] for slot in END_SLOTS],
+                blocks[far_end, term, extra_rows, :],
+            )
+
+        @pl.loop(0, groups)
+        def _(group):
+            add_far(
+                [end_rows(slot, group, slice(None)) for slot in END_SLOTS],
+                far_blocks(far_end, group),
+            )
+
+        for index, slot in enumerate(END_SLOTS):
+            stage_end[index, far_end] = acc_end[slot, far_end].astype(BF16)
+
+        for first in (True, False):
+            for index in range(4):
+                @pl.when(goes(index) & (across(index) == first))
+                def _():
+                    part_end_copy(index, far_end).start()
+
         send_parts(far_end)
 
-        for index in range(4):
+        @pl.loop(cut, terms)
+        def _(term):
+            extra_copy(home, term, me).wait_recv()
+            extra_multiply(home, [0, 1, 2, 3], term)
+
+        def home_strip(part):
             @pl.loop(0, groups)
             def _(group):
-                end_multiply(OFFSETS[index] + 2, group, far_end)
-
-            send_end_parts(index, far_end)
-
-        @pl.loop(0, groups)
-        def _(group):
-            end_copy(home, group, me).wait_recv()
-
-            @pl.loop(0, 4)
-            def _(owner):
-                end_multiply(home, group, owner)
+                home_copy(part, group, me).wait_recv()
+
+                spot = pl.ds(pl.multiple_of(part * strip, strip), strip)
+                end_multiply(home, group, [0, 1, 2, 3], spot)
+
+        def send_back(part):
+            spot = pl.ds(pl.multiple_of(part * strip, strip), strip)
+            back[:, spot, :] = acc_end[home, :, spot, :].astype(BF16)
+            back_copy(part, near_end).start()
+
+        home_strip(0)
 
         for index in range(4):
             @pl.when(comes(index))
@@ -431,8 +592,12 @@
                     part_end_copy(index, owner).wait_recv()
                     acc_end[home, owner] += landed_end[index, owner].astype(F32)
 
-        back[...] = acc_end[home].astype(BF16)
-        back_copy(near_end).start()
+        send_back(0)
+
+        @pl.loop(1, strips)
+        def _(part):
+            home_strip(part)
+            send_back(part)
 
         @pl.loop(0, 4)
         def _(owner):
@@ -449,41 +614,51 @@
         def _(rank):
             mask_rows(me + turn * rank)
 
-        def multiply(owner, term, block):
-            acc[owner] += jnp.dot(comb[term, :, near_rows], block, preferred_element_type=F32)
-
-        @pl.loop(0, terms)
-        def _(term):
-            multiply(me, term, block_of(me, term, near_rows))
+        def multiply(owner, term, block, spot):
+            acc[owner] += jnp.dot(comb[term, :, spot], block, preferred_element_type=F32)
+
+        @pl.loop(0, cut)
+        def _(term):
+            multiply(me, term, block_of(me, term, near_rows), near_rows)
+
+        @pl.loop(cut, terms)
+        def _(term):
+            multiply(me, term, block_of(me, term, short_rows), short_rows)
 
         send_parts(me)
-
-        @pl.loop(0, early)
-        def _(term):
-            arrived(near_mid, term)
-            multiply(near_mid, term, block_of(near_mid, term, near_rows))
 
         @pl.loop(1, 4)
         def _(rank):
             owner = me + turn * rank
 
-            @pl.loop(jnp.where(rank == 1, early, 0), terms)
+            @pl.loop(0, cut)
             def _(term):
-                block_arrived(owner, term)
-                multiply(owner, term, blocks[owner, term, near_rows, :])
+                block_arrived(owner, term, near_rows)
+                multiply(owner, term, blocks[owner, term, near_rows, :], near_rows)
+
+            @pl.loop(cut, terms)
+            def _(term):
+                block_arrived(owner, term, short_rows)
+                multiply(owner, term, blocks[owner, term, short_rows, :], short_rows)
 
             send_parts(owner)
 
-        @pl.loop(0, 4)
+        @pl.loop(0, 3)
         def _(rank):
             take_parts(me + turn * rank)
 
-        back_copy(me).wait_recv()
+        @pl.loop(0, strips)
+        def _(part):
+            back_copy(part, me).wait_recv()
+
         acc[:, home * rows:(home + 1) * rows, :] += back_landed[...].astype(F32)
 
-        @pl.loop(0, 4)
-        def _(owner):
-            write_out(owner)
+        @pl.loop(0, 3)
+        def _(rank):
+            write_out(me + turn * rank)
+
+        take_parts(far_end)
+        write_out(far_end)
 
     for index in range(4):
         @pl.when(goes(index))
@@ -498,40 +673,66 @@
 
     @pl.when(is_mid)
     def _():
-        state_own(0, near_end).wait_send()
-        state_own(1, other_mid).wait_send()
-        state_relay(2, other_mid, near_end).wait_send()
-        state_relay(3, near_end, other_mid).wait_send()
-
-        @pl.loop(0, early)
-        def _(term):
-            own_copy(1, term, near_end).wait_send()
-
-        @pl.loop(early, terms)
-        def _(term):
-            block_copy(own_send, 1, me, term, near_end).wait_send()
+        for part in range(2):
+            state_copy(0, me, part, near_end).wait_send()
+            state_copy(1, me, part, other_mid).wait_send()
+            state_copy(2, other_mid, part, near_end).wait_send()
+            state_copy(3, near_end, part, other_mid).wait_send()
 
         @pl.loop(0, terms)
         def _(term):
-            own_copy(0, term, other_mid).wait_send()
-            relay_copy(1, near_end, term, other_mid).wait_send()
-            block_copy(relay_send, 0, other_mid, term, near_end).wait_send()
-            block_copy(relay_send, 2, far_end, term, near_end).wait_send()
-
-        back_copy(near_end).wait_send()
+            own_copy(term, other_mid).wait_send()
+            relay_copy(near_end, term, other_mid).wait_send()
+            turns = jnp.logical_not(edge) & (term >= turned)
+
+            @pl.when(turns)
+            def _():
+                turn_off(term).wait_send()
+
+            @pl.when(edge & (term >= turned))
+            def _():
+                pass_on(term).wait_send()
+
+            @pl.when(jnp.logical_not(turns))
+            def _():
+                sent_block(own_send, 1, me, term)
+
+            sent_block(relay_send, 0, other_mid, term)
+            sent_block(relay_send, 2, far_end, term)
+
+        @pl.loop(0, strips)
+        def _(part):
+            back_copy(part, near_end).wait_send()
 
     @pl.when(is_end)
     def _():
-        state_own(0, near_mid).wait_send()
+        for part in range(2):
+            state_copy(0, me, part, near_mid).wait_send()
 
         @pl.loop(0, terms)
         def _(term):
-            own_copy(0, term, near_mid).wait_send()
-
-        for slot in END_SLOTS:
+            own_copy(term, near_mid).wait_send()
+
+        for index, slot in enumerate(END_SLOTS):
+            @pl.when(goes(index))
+            def _():
+                @pl.loop(cut, terms)
+                def _(term):
+                    extra_copy(slot, term, near_mid).wait_send()
+
+                @pl.loop(0, groups)
+                def _(group):
+                    end_copy(slot, group, near_mid).wait_send()
+
+        @pl.loop(cut, terms)
+        def _(term):
+            extra_copy(home, term, near_mid).wait_send()
+
+        @pl.loop(0, strips)
+        def _(part):
             @pl.loop(0, groups)
             def _(group):
-                end_copy(slot, group, near_mid).wait_send()
+                home_copy(part, group, near_mid).wait_send()
 
 
 def line_apply(sectors, slots, dims, channel_term, channel_out, coefs, state, right, left):
@@ -541,11 +742,13 @@
     cells = slots * terms
     per = 4
     groups = terms // per
+    strips = 2
+    detours, extras, least = (2, 5, 0) if sectors == 8 and terms == 16 else (0, 1, 1)
     tall = slots * rows
     dma = pltpu.SemaphoreType.DMA
     any_space = pl.BlockSpec(memory_space=pl.ANY)
     return pl.pallas_call(
-        functools.partial(line_kernel, sectors),
+        functools.partial(line_kernel, sectors, detours, least),
         out_shape=pltpu.VMEM((rows, width), F32),
         in_specs=[any_space] * 7,
         out_specs=pl.BlockSpec(memory_space=pltpu.VMEM),
@@ -568,6 +771,8 @@
             pltpu.VMEM((4, terms, width, cols), BF16),
             pltpu.VMEM((terms, tall, width), BF16),
             pltpu.VMEM((slots, groups, per, rows, rows), BF16),
+            pltpu.VMEM((slots, extras, rows, rows), BF16),
+            pltpu.VMEM((max(detours, 1), width - rows, cols), BF16),
             pltpu.VMEM((4, tall, cols), F32),
             pltpu.VMEM((slots, 4, rows, cols), F32),
             pltpu.VMEM((4, 4, rows, cols), BF16),
@@ -576,10 +781,12 @@
             pltpu.VMEM((4, 4, rows, cols), BF16),
             pltpu.VMEM((4, rows, cols), BF16),
             pltpu.VMEM((4, rows, cols), BF16),
-            dma((8,)), dma((4,)), dma((4,)),
+            dma((8,)), dma((4, 2)), dma((4, 2)),
             dma((2, terms)), dma((3, terms)), dma((4, terms)),
-            dma((slots, groups)), dma((slots, groups)),
-            dma((4, 4)), dma((4, 4)), dma((4, 4)), dma((4, 4)), dma((2,)),
+            dma((slots, groups)), dma((slots, groups)), dma((slots, extras)), dma((slots, extras)),
+            dma((strips, groups)), dma((strips, groups)),
+            dma((2, max(detours, 1))), dma((max(detours, 1),)),
+            dma((4, 4)), dma((4, 4)), dma((4, 4)), dma((4, 4)), dma((2, strips)),
         ],
         compiler_params=pltpu.CompilerParams(
             has_side_effects=True, collective_id=0, vmem_limit_bytes=60 * 2**20

time: 122 us -> 119 us (0.975)
  Pallas kernels: 120 us -> 117 us
    pallas_call x1, Pallas kernels: 120 us -> 117 us  [line_apply(): pl.pallas_call(functools.partial(line_kernel, sectors, detours, least), o...]
where the time goes in v4:
time: 119 us
  Pallas kernels  117 us (98%)
    pallas_call x1, Pallas kernels, line_apply(): pl.pallas_call(functools.partial(line_kernel, sectors, detours, least), o...  117 us

profile of v4, /device:TPU:0, one launch (start us, length us, event | category | flops | bytes accessed | tf_op | source)
XLA Modules:
  0.0 118.7 jit_solution(2280775904364494076)
XLA Ops:
  0.7 117.2 %shard_map.73 = f32[128,512]{1,0:T(8,128)S(1)} custom-call(s32[1]{0:T(128)} %copy.8.dims_ref, s32[72]{0:T(128)} %term_ref.1, s32[72]{0:T(128)} %out_id_ref.1, bf16[72]{0:T(256)(128)(2,1)} %coef_ref.1, bf16[128,512]{1,0:T(8,128)(2,1)} %bitcast.8, bf16[16,512,128]{2,1,0:T(8,128)(2,1)} %bitcast.7, bf16[72,128,512]{2,1,0:T(8,128)(2,1)} %left_ref.1), custom_call_target="tpu_custom_call" | custom-call | tf_op jit(solution)/shard_map/pallas_call | solution.py:750
  117.9 0.8 select_bitcast_fusion
  (2 shorter events, 0.0 us)

commit v5 on v4

--- a/solution.py
+++ b/solution.py
@@ -446,9 +446,26 @@
         rights = [far_blocks(owner, group) for owner in owners]
         add_end(slot, owners, spot, end_rows(slot, group, spot), rights)
 
-    def extra_multiply(slot, owners, term):
-        rights = [blocks[owner, term, extra_rows, :] for owner in owners]
-        add_end(slot, owners, slice(None), comb_extra[slot, terms - 1 - term], rights)
+    extras = comb_extra.shape[1]
+    has_extras = edge | (least > 0)
+
+    def extra_left(slot):
+        return jnp.concatenate([comb_extra[slot, index] for index in range(extras)], axis=1)
+
+    def extra_right(owner):
+        return jnp.concatenate(
+            [blocks[owner, terms - 1 - index, extra_rows, :] for index in range(extras)], axis=0
+        )
+
+    def extra_multiply(slot, owners):
+        @pl.loop(cut, terms)
+        def _(term):
+            extra_copy(slot, term, me).wait_recv()
+
+        @pl.when(has_extras)
+        def _():
+            rights = [extra_right(owner) for owner in owners]
+            add_end(slot, owners, slice(None), extra_left(slot), rights)
 
     def add_far(left, right):
         product = jnp.dot(
@@ -472,6 +489,12 @@
             acc[owner] += jnp.dot(comb[term], blocks[owner, term], preferred_element_type=F32)
 
         near_three = [me, other_mid, near_end]
+
+        def add_far_group(group):
+            add_far(
+                [end_rows(slot, group, slice(None)) for slot in END_SLOTS],
+                far_blocks(far_end, group),
+            )
 
         for index, slot in enumerate(END_SLOTS):
             @pl.when(jnp.logical_not(goes(index)))
@@ -517,17 +540,17 @@
             arrived(far_end, term)
             blocks[far_end, term] = block_of(far_end, term, everything)
             send_block(relay_send, 2, far_end, term)
-            multiply(far_end, term)
+
+            @pl.when(term < terms - 1)
+            def _():
+                multiply(far_end, term)
 
             for index in range(4):
                 slot = OFFSETS[index] + 2
 
                 @pl.when((term == (index + 1) * terms // 4 - 2) & goes(index))
                 def _():
-                    @pl.loop(cut, terms)
-                    def _(late):
-                        extra_copy(slot, late, me).wait_recv()
-                        extra_multiply(slot, near_three, late)
+                    extra_multiply(slot, near_three)
 
                     @pl.loop(0, groups)
                     def _(group):
@@ -539,19 +562,17 @@
                     def _(which):
                         send_end_parts(index, near_owner(which))
 
-        @pl.loop(cut, terms)
-        def _(term):
-            add_far(
-                [comb_extra[slot, terms - 1 - term] for slot in END_SLOTS],
-                blocks[far_end, term, extra_rows, :],
-            )
-
-        @pl.loop(0, groups)
-        def _(group):
-            add_far(
-                [end_rows(slot, group, slice(None)) for slot in END_SLOTS],
-                far_blocks(far_end, group),
-            )
+            @pl.when(term == terms - 2)
+            def _():
+                @pl.loop(0, groups - 1)
+                def _(group):
+                    add_far_group(group)
+
+        add_far_group(groups - 1)
+
+        @pl.when(has_extras)
+        def _():
+            add_far([extra_left(slot) for slot in END_SLOTS], extra_right(far_end))
 
         for index, slot in enumerate(END_SLOTS):
             stage_end[index, far_end] = acc_end[slot, far_end].astype(BF16)
@@ -562,12 +583,9 @@
                 def _():
                     part_end_copy(index, far_end).start()
 
-        send_parts(far_end)
-
-        @pl.loop(cut, terms)
-        def _(term):
-            extra_copy(home, term, me).wait_recv()
-            extra_multiply(home, [0, 1, 2, 3], term)
+        multiply(far_end, terms - 1)
+
+        extra_multiply(home, [0, 1, 2, 3])
 
         def home_strip(part):
             @pl.loop(0, groups)
@@ -593,6 +611,7 @@
                     acc_end[home, owner] += landed_end[index, owner].astype(F32)
 
         send_back(0)
+        send_parts(far_end)
 
         @pl.loop(1, strips)
         def _(part):
@@ -743,7 +762,7 @@
     per = 4
     groups = terms // per
     strips = 2
-    detours, extras, least = (2, 5, 0) if sectors == 8 and terms == 16 else (0, 1, 1)
+    detours, extras, least = (3, 6, 0) if sectors == 8 and terms == 16 else (0, 1, 1)
     tall = slots * rows
     dma = pltpu.SemaphoreType.DMA
     any_space = pl.BlockSpec(memory_space=pl.ANY)

time: 119 us -> 118 us (level)
    pallas_call x1, Pallas kernels: 117 us -> 116 us  [line_apply(): pl.pallas_call(functools.partial(line_kernel, sectors, detours, least), o...]
where the time goes in v5:
time: 118 us; the launch traced here: 117 us
  Pallas kernels  116 us (98%)
    pallas_call x1, Pallas kernels, line_apply(): pl.pallas_call(functools.partial(line_kernel, sectors, detours, least), o...  116 us

profile of v5, /device:TPU:0, one launch (start us, length us, event | category | flops | bytes accessed | tf_op | source)
XLA Modules:
  0.0 117.4 jit_solution(3017827732860711467)
XLA Ops:
  0.7 115.9 %shard_map.73 = f32[128,512]{1,0:T(8,128)S(1)} custom-call(s32[1]{0:T(128)} %copy.8.dims_ref, s32[72]{0:T(128)} %term_ref.1, s32[72]{0:T(128)} %out_id_ref.1, bf16[72]{0:T(256)(128)(2,1)} %coef_ref.1, bf16[128,512]{1,0:T(8,128)(2,1)} %bitcast.8, bf16[16,512,128]{2,1,0:T(8,128)(2,1)} %bitcast.7, bf16[72,128,512]{2,1,0:T(8,128)(2,1)} %left_ref.1), custom_call_target="tpu_custom_call" | custom-call | tf_op jit(solution)/shard_map/pallas_call | solution.py:769
  116.6 0.8 select_bitcast_fusion
  (2 shorter events, 0.0 us)

commit v6 on v5

--- a/solution.py
+++ b/solution.py
@@ -600,16 +600,19 @@
             back[:, spot, :] = acc_end[home, :, spot, :].astype(BF16)
             back_copy(part, near_end).start()
 
-        home_strip(0)
-
-        for index in range(4):
-            @pl.when(comes(index))
-            def _():
-                @pl.loop(0, 4)
-                def _(owner):
+        def take_end_parts(owner):
+            for index in range(4):
+                @pl.when(comes(index))
+                def _():
                     part_end_copy(index, owner).wait_recv()
                     acc_end[home, owner] += landed_end[index, owner].astype(F32)
 
+        @pl.loop(0, 3)
+        def _(which):
+            take_end_parts(near_owner(which))
+
+        home_strip(0)
+        take_end_parts(far_end)
         send_back(0)
         send_parts(far_end)
 

time: 118 us -> 118 us (level)
  no operation moved by 1% of the time
where the time goes in v6:
time: 118 us; the launch traced here: 117 us
  Pallas kernels  116 us (98%)
    pallas_call x1, Pallas kernels, line_apply(): pl.pallas_call(functools.partial(line_kernel, sectors, detours, least), o...  116 us

profile of v6, /device:TPU:0, one launch (start us, length us, event | category | flops | bytes accessed | tf_op | source)
XLA Modules:
  0.0 117.4 jit_solution(12452325624933649756)
XLA Ops:
  0.7 115.9 %shard_map.73 = f32[128,512]{1,0:T(8,128)S(1)} custom-call(s32[1]{0:T(128)} %copy.8.dims_ref, s32[72]{0:T(128)} %term_ref.1, s32[72]{0:T(128)} %out_id_ref.1, bf16[72]{0:T(256)(128)(2,1)} %coef_ref.1, bf16[128,512]{1,0:T(8,128)(2,1)} %bitcast.8, bf16[16,512,128]{2,1,0:T(8,128)(2,1)} %bitcast.7, bf16[72,128,512]{2,1,0:T(8,128)(2,1)} %left_ref.1), custom_call_target="tpu_custom_call" | custom-call | tf_op jit(solution)/shard_map/pallas_call | solution.py:772
  116.6 0.8 select_bitcast_fusion
  (2 shorter events, 0.0 us)
